TPU v7x, 32 devices: a whole 2x2x4 slice. The times are simulated.
32 devices in a mesh: sfc: 16 (over z, x, core), lvl: 2 (over y).
Axes of the slice: x: 2, y: 2, z: 4, core: 2. Of those that a mesh axis runs over, the one named last changes fastest.
Arguments:
- right_side: float32 [16384, 128], P(('sfc', 'lvl')), may hold values from -48 to 48
- cell_coef: float32 [16384], P(('sfc', 'lvl')), may hold values from 4 to 16
- fine_count: int32 [32], replicated, may hold values from 256 to 512, as said below
- cell_matrix: float32 [128, 128], replicated, may hold values from -0.5 to 0.5
- face_near: float32 [128, 128], replicated, may hold values from -0.5 to 0.5
- face_far: float32 [128, 128], replicated, may hold values from -0.5 to 0.5
- prolong: float32 [8, 128, 128], replicated, may hold values from -0.5 to 0.5
Outputs:
- solution: float32 [16384, 128], P(('sfc', 'lvl'))
Inputs may be any that keep to these rules, and one draw needn't show every extreme that they name: `fine_count`: each device's count is a multiple of 8 and at least 256; exactly one device holds 512, every other at most 504.
All inputs are finite; a program needn't handle non-finite values.
Results may differ from a plain program's by a relative error of at most 0.000051.
Values sent between devices are 32-bit elements; how exact they have to be, the bound alone decides.
No kernel may reach another device: no remote copies, remote signals or barrier semaphores. Data moves between devices by JAX's collectives and lax.ppermute only.
A program may use at most 64 MiB of HBM per device.

v0:
```python
import jax
import jax.numpy as jnp
from jax import lax
from jax.sharding import PartitionSpec as P

DEG = 3


def padded_2(cells, sides, width):
    for axis, dim in sides:
        count = lax.axis_size(axis)
        ends = count - 1
        head = lax.slice_in_dim(cells, 0, width, axis=dim)
        tail = lax.slice_in_dim(cells, cells.shape[dim] - width, cells.shape[dim], axis=dim)
        cells = jnp.concatenate(
            [
                lax.ppermute(tail, axis, [(i, (i + 1) % count) for i in range(ends)]),
                cells,
                lax.ppermute(head, axis, [((i + 1) % count, i) for i in range(ends)]),
            ],
            axis=dim,
        )
    return cells


def chain_apply(field, chain_coef, is_live, live_count, stride, ghosts, coupling):
    capacity = field.shape[0]
    tail_rows = lax.dynamic_slice_in_dim(field, live_count - stride, stride, 0)
    rim_rows = jnp.concatenate([field[:stride], tail_rows], 0)
    extended = ghosts(rim_rows)
    ghost_prev = extended[:stride]
    ghost_next = extended[3 * stride :]
    buffer = jnp.concatenate(
        [ghost_prev, field, jnp.zeros((stride, field.shape[1]), jnp.float32)], 0
    )
    buffer = lax.dynamic_update_slice_in_dim(buffer, ghost_next, stride + live_count, 0)
    joined = jnp.concatenate(
        [
            field,
            buffer[stride + 1 : stride + 1 + capacity],
            buffer[stride - 1 : stride - 1 + capacity],
            buffer[2 * stride : 2 * stride + capacity],
            buffer[:capacity],
        ],
        1,
    )
    result = chain_coef[:, None] * field + jnp.dot(
        joined, coupling, precision=lax.Precision.HIGHEST, preferred_element_type=jnp.float32
    )
    return jnp.where(is_live[:, None], result, 0.0)


def local_apply(field, chain_coef, is_live, stride, coupling):
    width = field.shape[1]
    zero_one = jnp.zeros((1, width), jnp.float32)
    zero_far = jnp.zeros((stride, width), jnp.float32)
    joined = jnp.concatenate(
        [
            field,
            jnp.concatenate([field[1:], zero_one], 0),
            jnp.concatenate([zero_one, field[:-1]], 0),
            jnp.concatenate([field[stride:], zero_far], 0),
            jnp.concatenate([zero_far, field[:-stride]], 0),
        ],
        1,
    )
    result = chain_coef[:, None] * field + jnp.dot(
        joined, coupling, precision=lax.Precision.HIGHEST, preferred_element_type=jnp.float32
    )
    return jnp.where(is_live[:, None], result, 0.0)


def rims_of(field, live_count, depth):
    tail_rows = lax.dynamic_slice_in_dim(field, live_count - depth, depth, 0)
    return jnp.concatenate([field[:depth], tail_rows], 0)


def widen(field, ghost_rows, live_count, depth):
    tail_zeros = jnp.zeros((depth,) + field.shape[1:], jnp.float32)
    buffer = jnp.concatenate([ghost_rows[:depth], field, tail_zeros], 0)
    return lax.dynamic_update_slice_in_dim(buffer, ghost_rows[3 * depth :], depth + live_count, 0)


def jacobi_scale(chain_coef, is_live, cell_diag):
    safe_coef = jnp.where(is_live, chain_coef, 16.0)
    return jnp.where(is_live[:, None], 1.0 / (safe_coef[:, None] + cell_diag[None, :]), 0.0)


def chebyshev(apply_fn, jacobi, source, start):
    center = 1.025
    radius = 0.775
    sigma_ratio = center / radius
    if start is None:
        residual = source
    else:
        residual = source - apply_fn(start)
    update = jacobi * residual / center
    iterate = update if start is None else start + update
    weight_prev = 1.0 / sigma_ratio
    for repeat in range(DEG - 1):
        weight_next = 1.0 / (2.0 * sigma_ratio - weight_prev)
        residual = source - apply_fn(iterate)
        update = weight_next * weight_prev * update + 2.0 * weight_next / radius * jacobi * residual
        iterate = iterate + update
        weight_prev = weight_next
    return iterate


def shards(right_side, cell_coef, fine_count, cell_matrix, face_near, face_far, prolong):
    capacity, values = right_side.shape
    stride = capacity // 16
    coarse_stride = capacity // 16
    coarse_slots = capacity // 8
    coupling = jnp.concatenate([cell_matrix, -face_near, -face_near.T, -face_far, -face_far.T], 0)
    cell_diag = jnp.diagonal(cell_matrix)
    device_index = lax.axis_index(("sfc", "lvl"))
    live_count = fine_count[device_index]
    is_live = jnp.arange(capacity, dtype=jnp.int32) < live_count
    source = jnp.where(is_live[:, None], right_side, 0.0)
    depth = 3 * stride
    chain_size = lax.axis_size(("sfc", "lvl"))
    wide_index = jnp.arange(capacity + 2 * depth, dtype=jnp.int32)
    has_prev = device_index > 0
    has_next = device_index < chain_size - 1
    wide_live = (
        (wide_index >= depth) & (wide_index < depth + live_count)
        | (wide_index < depth) & has_prev
        | (wide_index >= depth + live_count) & (wide_index < 2 * depth + live_count) & has_next
    )
    own_coef = jnp.where(is_live, cell_coef, 0.0)
    source_ghosts = padded_2(rims_of(source, live_count, depth), ((("sfc", "lvl"), 0),), depth)
    coef_ghosts = padded_2(rims_of(own_coef, live_count, depth), ((("sfc", "lvl"), 0),), depth)
    wide_source = widen(source, source_ghosts, live_count, depth)
    wide_coef = widen(own_coef, coef_ghosts, live_count, depth)
    wide_jacobi = jacobi_scale(wide_coef, wide_live, cell_diag)

    def wide_apply(field):
        return local_apply(field, wide_coef, wide_live, stride, coupling)

    wide_iterate = chebyshev(wide_apply, wide_jacobi, wide_source, None)
    wide_residual = wide_source - wide_apply(wide_iterate)
    iterate = jnp.where(is_live[:, None], wide_iterate[depth : depth + capacity], 0.0)
    residual = jnp.where(is_live[:, None], wide_residual[depth : depth + capacity], 0.0)
    restrict_map = jnp.transpose(prolong, (0, 2, 1)).reshape(8 * values, values)
    coarse_source = jnp.dot(
        residual.reshape(coarse_slots, 8 * values),
        restrict_map,
        precision=lax.Precision.HIGHEST,
        preferred_element_type=jnp.float32,
    )
    coarse_coef = jnp.mean(cell_coef.reshape(coarse_slots, 8), axis=1)
    coarse_count = live_count // 8
    group_size = lax.axis_size("lvl")
    lvl_index = lax.axis_index("lvl")
    sfc_index = lax.axis_index("sfc")
    pieces, coef_pieces = (
        lax.all_gather(coarse_source, "lvl", axis=0, tiled=True),
        lax.all_gather(coarse_coef, "lvl", axis=0, tiled=True),
    )
    member_counts = lax.dynamic_slice_in_dim(fine_count, sfc_index * group_size, group_size) // 8
    buffer = jnp.zeros(((group_size + 1) * coarse_slots, values), jnp.float32)
    coef_buffer = jnp.zeros(((group_size + 1) * coarse_slots,), jnp.float32)
    offset = jnp.zeros((), jnp.int32)
    for member in range(group_size):
        lower = member * coarse_slots
        buffer = lax.dynamic_update_slice_in_dim(
            buffer, pieces[lower : lower + coarse_slots], offset, 0
        )
        coef_buffer = lax.dynamic_update_slice_in_dim(
            coef_buffer, coef_pieces[lower : lower + coarse_slots], offset, 0
        )
        offset = offset + member_counts[member]
    group_slots = group_size * coarse_slots
    group_source = buffer[:group_slots]
    group_coef = coef_buffer[:group_slots]
    is_group_live = jnp.arange(group_slots, dtype=jnp.int32) < offset
    group_jacobi = jacobi_scale(group_coef, is_group_live, cell_diag)

    def coarse_ghosts(rim_rows):
        return padded_2(rim_rows, (("sfc", 0),), coarse_stride)

    def group_apply(field):
        return chain_apply(
            field, group_coef, is_group_live, offset, coarse_stride, coarse_ghosts, coupling
        )

    group_solution = chebyshev(group_apply, group_jacobi, group_source, None)
    own_offset = jnp.sum(
        jnp.where(jnp.arange(group_size, dtype=jnp.int32) < lvl_index, member_counts, 0)
    )
    padded = jnp.concatenate([group_solution, jnp.zeros((coarse_slots, values), jnp.float32)], 0)
    own_rows = lax.dynamic_slice_in_dim(padded, own_offset, coarse_slots, 0)
    is_coarse = jnp.arange(coarse_slots, dtype=jnp.int32) < coarse_count
    correction = jnp.where(is_coarse[:, None], own_rows, 0.0)
    prolong_map = jnp.transpose(prolong, (1, 0, 2)).reshape(values, 8 * values)
    corrected = iterate + jnp.dot(
        correction, prolong_map, precision=lax.Precision.HIGHEST, preferred_element_type=jnp.float32
    ).reshape(capacity, values)
    start_ghosts = padded_2(rims_of(corrected, live_count, depth), ((("sfc", "lvl"), 0),), depth)
    wide_start = widen(corrected, start_ghosts, live_count, depth)
    wide_final = chebyshev(wide_apply, wide_jacobi, wide_source, wide_start)
    return jnp.where(is_live[:, None], wide_final[depth : depth + capacity], 0.0)


def solution(mesh):
    placed = (P(("sfc", "lvl"), None), P(("sfc", "lvl")), P(), P(), P(), P(), P())
    return jax.shard_map(
        shards, mesh=mesh, in_specs=placed, out_specs=P(("sfc", "lvl"), None), check_vma=False
    )
```

profile of v0, /device:TPU:15, one launch (start us, length us, event | category | flops | bytes accessed | tf_op | source)
XLA Modules:
  0.0 92.3 jit_solution(17129813842159177328)
XLA Ops:
  0.0 1.3 %dynamic_slice.24 = s32[1]{0:T(128)} dynamic-slice(s32[32]{0:T(128)} %param.9, s32[]{:T(128)S(6)} %select_n.110), dynamic_slice_sizes={1} | dynamic-slice | bytes 12 | tf_op jit(solution)/shard_map/dynamic_slice | solution.py:117
  1.3 1.3 %broadcast_select_fusion.2 = f32[512]{0:T(512)S(1)} fusion(f32[512]{0:T(512)} %param.8, s32[]{:T(128)} %bitcast), kind=kLoop, calls=%fused_computation.116 | loop fusion | flops 1024 | bytes 4100 | tf_op jit(solution)/shard_map/jit(_where)/select_n | solution.py:130
  4.0 3.7 %collective-permute-start = (f32[96]{0:T(128)S(1)}, f32[96]{0:T(128)S(1)}, u32[]{:S(2)}, u32[]{:S(2)}) collective-permute-start(f32[96]{0:T(128)S(1)} %get-tuple-element.63), channel_id=1, source_target_pairs={{0,1},{1,2},{2,3},{3,4},{4,5},{5,6},{6,7},{7,8},{8,9},{9,10},{10,1... | collective-permute-start | bytes 1160 | tf_op jit(solution)/shard_map/ppermute | solution.py:17
  7.7 1.9 %collective-permute-start.1 = (f32[96]{0:T(128)S(1)}, f32[96]{0:T(128)S(1)}, u32[]{:S(2)}, u32[]{:S(2)}) collective-permute-start(f32[96]{0:T(128)S(1)} %get-tuple-element.62), channel_id=1, source_target_pairs={{1,0},{2,1},{3,2},{4,3},{5,4},{6,5},{7,6},{8,7},{9,8},{10,9},{11,1... | collective-permute-start | bytes 1160 | tf_op jit(solution)/shard_map/ppermute | solution.py:19
  9.6 0.7 iota_compare_fusion.5
  10.3 1.1 %broadcast_select_fusion = f32[512,128]{1,0:T(8,128)S(1)} fusion(f32[512,128]{1,0:T(8,128)} %param.7, pred[512]{0:T(512)(128)(4,1)S(1)} %iota_compare_fusion.5), kind=kLoop, calls=%fused_computation.60 | loop fusion | flops 65536 | bytes 524800 | tf_op jit(solution)/shard_map/jit(_where)/select_n | solution.py:119
  11.4 5.4 %collective-permute-start.2 = (f32[96,128]{1,0:T(8,128)S(1)}, f32[96,128]{1,0:T(8,128)S(1)}, u32[]{:S(2)}, u32[]{:S(2)}) collective-permute-start(f32[96,128]{1,0:T(8,128)S(1)} %get-tuple-element.51), channel_id=1, source_target_pairs={{0,1},{1,2},{2,3},{3,4},{4,5},{5,6},{6,7},{7,8},{8,9},{9,10},{10,1... | collective-permute-start | bytes 147464 | tf_op jit(solution)/shard_map/ppermute | solution.py:17
  16.9 1.9 %collective-permute-start.3 = (f32[96,128]{1,0:T(8,128)S(1)}, f32[96,128]{1,0:T(8,128)S(1)}, u32[]{:S(2)}, u32[]{:S(2)}) collective-permute-start(f32[96,128]{1,0:T(8,128)S(1)} %get-tuple-element.50), channel_id=1, source_target_pairs={{1,0},{2,1},{3,2},{4,3},{5,4},{6,5},{7,6},{8,7},{9,8},{10,9},{11,1... | collective-permute-start | bytes 147464 | tf_op jit(solution)/shard_map/ppermute | solution.py:19
  18.8 1.4 %fusion.28 = (s32[]{:T(128)}, s32[2]{0:T(128)S(1)}) fusion(s32[]{:T(128)S(6)} %axis_index.14, s32[32]{0:T(128)} %param.9, s32[]{:T(128)S(6)} %select_n.121), kind=kLoop, calls=%fused_computation.117 | loop fusion | flops 35 | bytes 28 | tf_op jit(solution)/shard_map/reduce_sum | solution.py:188
  20.9 0.6 fusion.53
  22.8 0.8 reshape.50
  26.2 1.2 %copy.14 = f32[8,128,128]{1,2,0:T(8,128)S(1)} copy(f32[8,128,128]{2,1,0:T(8,128)} %param.13) | data formatting | bytes 1048576 | tf_op args[6]
  27.4 1.2 %gather_fusion = f32[128]{0:T(128)S(1)} fusion(f32[128,128]{1,0:T(8,128)S(1)} %copy-done, s32[128]{0:T(128)S(1)} %or_bitcast_fusion), kind=kCustom, calls=%fused_computation | custom fusion | bytes 2048 | tf_op jit(solution)/shard_map/jit(diagonal)/cond/branch_0_fun/gather | solution.py:115
  29.1 0.6 dynamic-slice
  30.5 3.9 %all-reduce.27 = f32[128]{0:T(128)S(1)} all-reduce(f32[128]{0:T(128)S(1)} %multiply_dynamic-update-slice_fusion), channel_id=1, replica_groups=mesh['sfc'=16,'lvl'=2] {'lvl'}, use_global_device_ids=true, to_apply=%add.27 | all-reduce | flops 128 | bytes 1024
  35.1 0.2 slice_dynamic-update-slice_fusion
  35.4 0.2 dynamic_update_slice.27
  35.7 0.2 maximum_maximum_fusion
  35.9 0.5 dynamic_update_slice.28
  36.4 0.3 constant_dynamic-update-slice_fusion
  36.9 1.8 %constant_dynamic-update-slice_fusion.6 = (f32[704,640]{1,0:T(8,128)S(1)}, f32[704,128]{1,0:T(8,128)S(1)}, f32[704,128]{1,0:T(8,128)S(1)}) fusion(f32[704,128]{1,0:T(8,128)S(1)} %get-tuple-element.19, f32[704,128]{1,0:T(8,128)S(1)} %dynamic_update_slice.28, f32[704]{0:T(1024)S(1)} %get-tuple-element.61, f32[128]{0:T(128)S(1)} %gather_fusion, ...), kind=kOutput, calls=%fused_computation.70 | convolution fusion | flops 693231616 | bytes 3939008 | tf_op jit(solution)/shard_map/dot_general | solution.py:67
  38.9 1.8 %constant_dynamic-update-slice_fusion.7 = (f32[704,640]{1,0:T(8,128)S(1)}, f32[704,128]{1,0:T(8,128)S(1)}, f32[704,128]{1,0:T(8,128)S(1)}) fusion(f32[704,128]{1,0:T(8,128)S(1)} %get-tuple-element.17, f32[704,128]{1,0:T(8,128)S(1)} %dynamic_update_slice.28, f32[704]{0:T(1024)S(1)} %dynamic_update_slice.27, f32[704,128]{1,0:T(8,128)S(1)} %get-tuple-element.71, ...), kind=kOutput, calls=%fused_computation.71 | convolution fusion | flops 693952512 | bytes 4302272 | tf_op jit(solution)/shard_map/dot_general | solution.py:67
  41.1 1.6 %fusion.55 = f32[704,128]{1,0:T(8,128)S(1)} fusion(f32[704,640]{1,0:T(8,128)S(1)} %pad_dynamic-update-slice_fusion.12, f32[640,128]{1,0:T(8,128)S(1)} %constant_dynamic-update-slice_fusion.1), kind=kOutput, calls=%fused_computation.149 | convolution fusion | flops 692060160 | bytes 2490368 | tf_op jit(solution)/shard_map/dot_general | solution.py:67
  42.7 0.3 fusion.15
  43.0 0.4 fusion.56
  43.4 3.4 %all_gather.7 = f32[128,128]{1,0:T(8,128)S(1)} all-gather(f32[64,128]{1,0:T(8,128)S(1)} %fusion.56), channel_id=1, replica_groups=mesh['sfc'=16,'lvl'=2] {'lvl'}, dimensions={0}, use_global_device_ids=true | all-gather | bytes 98304 | tf_op jit(solution)/shard_map/all_gather | solution.py:157
  46.9 0.3 dynamic_update_slice.32
  47.4 6.1 %collective-permute-start.4 = (f32[32,128]{1,0:T(8,128)S(1)}, f32[32,128]{1,0:T(8,128)S(1)}, u32[]{:S(2)}, u32[]{:S(2)}) collective-permute-start(f32[32,128]{1,0:T(8,128)S(1)} %get-tuple-element.55), channel_id=1, source_target_pairs={{0,2},{2,4},{4,6},{6,8},{8,10},{10,12},{12,14},{14,16},{16,18},{18... | collective-permute-start | bytes 49160 | tf_op jit(solution)/shard_map/ppermute | solution.py:17
  56.2 1.9 %collective-permute-start.5 = (f32[32,128]{1,0:T(8,128)S(1)}, f32[32,128]{1,0:T(8,128)S(1)}, u32[]{:S(2)}, u32[]{:S(2)}) collective-permute-start(f32[32,128]{1,0:T(8,128)S(1)} %get-tuple-element.54), channel_id=1, source_target_pairs={{2,0},{4,2},{6,4},{8,6},{10,8},{12,10},{14,12},{16,14},{18,16},{20... | collective-permute-start | bytes 49160 | tf_op jit(solution)/shard_map/ppermute | solution.py:19
  58.2 3.9 %collective-permute-done.5 = f32[32,128]{1,0:T(8,128)S(1)} collective-permute-done((f32[32,128]{1,0:T(8,128)S(1)}, f32[32,128]{1,0:T(8,128)S(1)}, u32[]{:S(2)}, u32[]{:S(2)}) %collective-permute-start.5) | collective-permute-done | bytes 16416 | tf_op jit(solution)/shard_map/ppermute | solution.py:19
  62.1 0.2 dynamic_update_slice.33
  62.3 0.5 constant_dynamic-update-slice_fusion.17
  62.8 1.9 %collective-permute-start.6 = (f32[32,128]{1,0:T(8,128)S(1)}, f32[32,128]{1,0:T(8,128)S(1)}, u32[]{:S(2)}, u32[]{:S(2)}) collective-permute-start(f32[32,128]{1,0:T(8,128)S(1)} %get-tuple-element.53), channel_id=1, source_target_pairs={{0,2},{2,4},{4,6},{6,8},{8,10},{10,12},{12,14},{14,16},{16,18},{18... | collective-permute-start | bytes 49160 | tf_op jit(solution)/shard_map/ppermute | solution.py:17
  66.8 2.4 %collective-permute-start.7 = (f32[32,128]{1,0:T(8,128)S(1)}, f32[32,128]{1,0:T(8,128)S(1)}, u32[]{:S(2)}, u32[]{:S(2)}) collective-permute-start(f32[32,128]{1,0:T(8,128)S(1)} %get-tuple-element.52), channel_id=1, source_target_pairs={{2,0},{4,2},{6,4},{8,6},{10,8},{12,10},{14,12},{16,14},{18,16},{20... | collective-permute-start | bytes 49160 | tf_op jit(solution)/shard_map/ppermute | solution.py:19
  69.3 3.4 %collective-permute-done.7 = f32[32,128]{1,0:T(8,128)S(1)} collective-permute-done((f32[32,128]{1,0:T(8,128)S(1)}, f32[32,128]{1,0:T(8,128)S(1)}, u32[]{:S(2)}, u32[]{:S(2)}) %collective-permute-start.7) | collective-permute-done | bytes 16416 | tf_op jit(solution)/shard_map/ppermute | solution.py:19
  72.8 0.2 dynamic_update_slice.34
  73.0 0.5 fusion.4
  73.4 0.7 fusion.17
  74.2 0.1 select_add_fusion
  74.4 3.4 %collective-permute-start.8 = (f32[96,128]{1,0:T(8,128)S(1)}, f32[96,128]{1,0:T(8,128)S(1)}, u32[]{:S(2)}, u32[]{:S(2)}) collective-permute-start(f32[96,128]{1,0:T(8,128)S(1)} %get-tuple-element.49), channel_id=1, source_target_pairs={{0,1},{1,2},{2,3},{3,4},{4,5},{5,6},{6,7},{7,8},{8,9},{9,10},{10,1... | collective-permute-start | bytes 147464 | tf_op jit(solution)/shard_map/ppermute | solution.py:17
  77.8 2.4 %collective-permute-start.9 = (f32[96,128]{1,0:T(8,128)S(1)}, f32[96,128]{1,0:T(8,128)S(1)}, u32[]{:S(2)}, u32[]{:S(2)}) collective-permute-start(f32[96,128]{1,0:T(8,128)S(1)} %get-tuple-element.48), channel_id=1, source_target_pairs={{1,0},{2,1},{3,2},{4,3},{5,4},{6,5},{7,6},{8,7},{9,8},{10,9},{11,1... | collective-permute-start | bytes 147464 | tf_op jit(solution)/shard_map/ppermute | solution.py:19
  80.2 0.2 maximum_maximum_fusion.1
  80.3 4.7 %collective-permute-done.9 = f32[96,128]{1,0:T(8,128)S(1)} collective-permute-done((f32[96,128]{1,0:T(8,128)S(1)}, f32[96,128]{1,0:T(8,128)S(1)}, u32[]{:S(2)}, u32[]{:S(2)}) %collective-permute-start.9) | collective-permute-done | bytes 49184 | tf_op jit(solution)/shard_map/ppermute | solution.py:19
  85.0 0.4 dynamic_update_slice.35
  85.7 1.8 %constant_dynamic-update-slice_fusion.19 = (f32[704,640]{1,0:T(8,128)S(1)}, f32[704,128]{1,0:T(8,128)S(1)}, f32[704,128]{1,0:T(8,128)S(1)}) fusion(f32[704,128]{1,0:T(8,128)S(1)} %dynamic_update_slice.35, f32[704,128]{1,0:T(8,128)S(1)} %dynamic_update_slice.28, f32[704]{0:T(1024)S(1)} %dynamic_update_slice.27, f32[128]{0:T(128)S(1)} %gather_fusion, ...), kind=kOutput, calls=%fused_computation.83 | convolution fusion | flops 692961280 | bytes 3939008 | tf_op jit(solution)/shard_map/dot_general | solution.py:67
  87.7 1.8 %broadcast_multiply_fusion = (f32[704,128]{1,0:T(8,128)S(1)}, f32[704,128]{1,0:T(8,128)S(1)}, f32[704,128]{1,0:T(8,128)S(1)}) fusion(f32[704]{0:T(1024)S(1)} %dynamic_update_slice.27, f32[704,128]{1,0:T(8,128)S(1)} %get-tuple-element.9, f32[704,128]{1,0:T(8,128)S(1)} %dynamic_update_slice.28, f32[704,128]{1,0:T(8,128)S(1)} %get-tuple-element.73, ...), kind=kOutput, calls=%fused_computation.58 | convolution fusion | flops 693682176 | bytes 4659904 | tf_op jit(solution)/shard_map/dot_general | solution.py:67
  89.8 1.6 %fusion.57 = f32[704,128]{1,0:T(8,128)S(1)} fusion(f32[704,640]{1,0:T(8,128)S(1)} %pad_dynamic-update-slice_fusion, f32[640,128]{1,0:T(8,128)S(1)} %constant_dynamic-update-slice_fusion.1), kind=kOutput, calls=%fused_computation.151 | convolution fusion | flops 692060160 | bytes 2490368 | tf_op jit(solution)/shard_map/dot_general | solution.py:67
  91.4 0.9 fusion.9
  (97 shorter events, 2.8 us)
Async XLA Ops:
  0.0 27.4 %copy-start = (f32[128,128]{1,0:T(8,128)S(1)}, f32[128,128]{1,0:T(8,128)}, u32[]{:S(2)}) copy-start(f32[128,128]{1,0:T(8,128)} %param.10) | copy-start | bytes 196612
  0.0 28.7 %copy-start.2 = (f32[128,128]{1,0:T(8,128)S(1)}, f32[128,128]{1,0:T(8,128)}, u32[]{:S(2)}) copy-start(f32[128,128]{1,0:T(8,128)} %param.11) | copy-start | bytes 196612
  0.0 28.9 %copy-start.1 = (f32[128,128]{1,0:T(8,128)S(1)}, f32[128,128]{1,0:T(8,128)}, u32[]{:S(2)}) copy-start(f32[128,128]{1,0:T(8,128)} %param.12) | copy-start | bytes 196612
  0.0 29.1 %copy-start.3 = (u32[32]{0:T(128)S(1)}, u32[32]{0:T(128)}, u32[]{:S(2)}) copy-start(u32[32]{0:T(128)} %constant.171) | copy-start | bytes 388
  4.0 31.3 %collective-permute-start = (f32[96]{0:T(128)S(1)}, f32[96]{0:T(128)S(1)}, u32[]{:S(2)}, u32[]{:S(2)}) collective-permute-start(f32[96]{0:T(128)S(1)} %get-tuple-element.63), channel_id=1, source_target_pairs={{0,1},{1,2},{2,3},{3,4},{4,5},{5,6},{6,7},{7,8},{8,9},{9,10},{10,1... | collective-permute-start | bytes 1160 | tf_op jit(solution)/shard_map/ppermute | solution.py:17
  7.7 27.7 %collective-permute-start.1 = (f32[96]{0:T(128)S(1)}, f32[96]{0:T(128)S(1)}, u32[]{:S(2)}, u32[]{:S(2)}) collective-permute-start(f32[96]{0:T(128)S(1)} %get-tuple-element.62), channel_id=1, source_target_pairs={{1,0},{2,1},{3,2},{4,3},{5,4},{6,5},{7,6},{8,7},{9,8},{10,9},{11,1... | collective-permute-start | bytes 1160 | tf_op jit(solution)/shard_map/ppermute | solution.py:19
  11.4 24.3 %collective-permute-start.2 = (f32[96,128]{1,0:T(8,128)S(1)}, f32[96,128]{1,0:T(8,128)S(1)}, u32[]{:S(2)}, u32[]{:S(2)}) collective-permute-start(f32[96,128]{1,0:T(8,128)S(1)} %get-tuple-element.51), channel_id=1, source_target_pairs={{0,1},{1,2},{2,3},{3,4},{4,5},{5,6},{6,7},{7,8},{8,9},{9,10},{10,1... | collective-permute-start | bytes 147464 | tf_op jit(solution)/shard_map/ppermute | solution.py:17
  16.9 19.0 %collective-permute-start.3 = (f32[96,128]{1,0:T(8,128)S(1)}, f32[96,128]{1,0:T(8,128)S(1)}, u32[]{:S(2)}, u32[]{:S(2)}) collective-permute-start(f32[96,128]{1,0:T(8,128)S(1)} %get-tuple-element.50), channel_id=1, source_target_pairs={{1,0},{2,1},{3,2},{4,3},{5,4},{6,5},{7,6},{8,7},{9,8},{10,9},{11,1... | collective-permute-start | bytes 147464 | tf_op jit(solution)/shard_map/ppermute | solution.py:19
  47.4 10.7 %collective-permute-start.4 = (f32[32,128]{1,0:T(8,128)S(1)}, f32[32,128]{1,0:T(8,128)S(1)}, u32[]{:S(2)}, u32[]{:S(2)}) collective-permute-start(f32[32,128]{1,0:T(8,128)S(1)} %get-tuple-element.55), channel_id=1, source_target_pairs={{0,2},{2,4},{4,6},{6,8},{8,10},{10,12},{12,14},{14,16},{16,18},{18... | collective-permute-start | bytes 49160 | tf_op jit(solution)/shard_map/ppermute | solution.py:17
  56.2 5.9 %collective-permute-start.5 = (f32[32,128]{1,0:T(8,128)S(1)}, f32[32,128]{1,0:T(8,128)S(1)}, u32[]{:S(2)}, u32[]{:S(2)}) collective-permute-start(f32[32,128]{1,0:T(8,128)S(1)} %get-tuple-element.54), channel_id=1, source_target_pairs={{2,0},{4,2},{6,4},{8,6},{10,8},{12,10},{14,12},{16,14},{18,16},{20... | collective-permute-start | bytes 49160 | tf_op jit(solution)/shard_map/ppermute | solution.py:19
  62.8 6.4 %collective-permute-start.6 = (f32[32,128]{1,0:T(8,128)S(1)}, f32[32,128]{1,0:T(8,128)S(1)}, u32[]{:S(2)}, u32[]{:S(2)}) collective-permute-start(f32[32,128]{1,0:T(8,128)S(1)} %get-tuple-element.53), channel_id=1, source_target_pairs={{0,2},{2,4},{4,6},{6,8},{8,10},{10,12},{12,14},{14,16},{16,18},{18... | collective-permute-start | bytes 49160 | tf_op jit(solution)/shard_map/ppermute | solution.py:17
  66.8 6.0 %collective-permute-start.7 = (f32[32,128]{1,0:T(8,128)S(1)}, f32[32,128]{1,0:T(8,128)S(1)}, u32[]{:S(2)}, u32[]{:S(2)}) collective-permute-start(f32[32,128]{1,0:T(8,128)S(1)} %get-tuple-element.52), channel_id=1, source_target_pairs={{2,0},{4,2},{6,4},{8,6},{10,8},{12,10},{14,12},{16,14},{18,16},{20... | collective-permute-start | bytes 49160 | tf_op jit(solution)/shard_map/ppermute | solution.py:19
  74.4 5.8 %collective-permute-start.8 = (f32[96,128]{1,0:T(8,128)S(1)}, f32[96,128]{1,0:T(8,128)S(1)}, u32[]{:S(2)}, u32[]{:S(2)}) collective-permute-start(f32[96,128]{1,0:T(8,128)S(1)} %get-tuple-element.49), channel_id=1, source_target_pairs={{0,1},{1,2},{2,3},{3,4},{4,5},{5,6},{6,7},{7,8},{8,9},{9,10},{10,1... | collective-permute-start | bytes 147464 | tf_op jit(solution)/shard_map/ppermute | solution.py:17
  77.8 7.2 %collective-permute-start.9 = (f32[96,128]{1,0:T(8,128)S(1)}, f32[96,128]{1,0:T(8,128)S(1)}, u32[]{:S(2)}, u32[]{:S(2)}) collective-permute-start(f32[96,128]{1,0:T(8,128)S(1)} %get-tuple-element.48), channel_id=1, source_target_pairs={{1,0},{2,1},{3,2},{4,3},{5,4},{6,5},{7,6},{8,7},{9,8},{10,9},{11,1... | collective-permute-start | bytes 147464 | tf_op jit(solution)/shard_map/ppermute | solution.py:19
where the time goes:
time: 93 us; the launch traced here: 92.3 us
  starting transfers between devices  31.1 us (33%)
  between operations  12.7 us (14%)
  matrix products  12.4 us (13%)
  waiting for transfers between devices  12.1 us (13%)
  local copies, waits for them, and re-layouts  9.72 us (10%)
  blocking collectives  7.35 us (8%)
  other arithmetic  7.02 us (8%)
    ppermute x5, starting transfers between devices, padded_2(): lax.ppermute(tail, axis, [(i, (i + 1) % count) for i in range(ends)])  20.5 us
    ppermute x5, waiting for transfers between devices, padded_2(): lax.ppermute(head, axis, [((i + 1) % count, i) for i in range(ends)])  12 us
    ppermute x5, starting transfers between devices, padded_2(): lax.ppermute(head, axis, [((i + 1) % count, i) for i in range(ends)])  10.5 us
    dot_general x6, matrix products, local_apply(): jnp.dot(joined, coupling, precision=lax.Precision.HIGHEST, preferred_elem...  10.4 us
    unnamed x1, blocking collectives  3.92 us
    all_gather x1, blocking collectives, shards(): lax.all_gather(coarse_source, 'lvl', axis=0, tiled=True)  3.43 us
    unnamed x40, local copies, waits for them, and re-layouts  2.53 us
  transfers between devices with their start and end apart: 10, of which 3 were waited for; matrix products, arithmetic and copies ran while one was open for 10% of the time, Pallas kernels for 0%

commit v1 on v0

v1 whole, which is shorter than its diff:
```python
import jax
import jax.numpy as jnp
from jax import lax
from jax.experimental import pallas as pl
from jax.experimental.pallas import tpu as pltpu
from jax.sharding import PartitionSpec as P

DEG = 3
AXES = ("sfc", "lvl")
CENTER = 1.025
RADIUS = 0.775
CHILDREN = 8


def chebyshev_weights():
    sigma = CENTER / RADIUS
    weight = 1.0 / sigma
    steps = [(0.0, 1.0 / CENTER)]
    for _ in range(DEG - 1):
        following = 1.0 / (2.0 * sigma - weight)
        steps.append((following * weight, 2.0 * following / RADIUS))
        weight = following
    return steps


STEPS = chebyshev_weights()


def step_weights(step):
    keep = jnp.float32(STEPS[0][0])
    gain = jnp.float32(STEPS[0][1])
    for index in range(1, DEG):
        keep = jnp.where(step == index, jnp.float32(STEPS[index][0]), keep)
        gain = jnp.where(step == index, jnp.float32(STEPS[index][1]), gain)
    return keep, gain


def device_number():
    return lax.axis_index("sfc") * lax.axis_size("lvl") + lax.axis_index("lvl")


def device_total():
    return lax.axis_size("sfc") * lax.axis_size("lvl")


def halves(value):
    high = value.astype(jnp.bfloat16)
    low = (value - high.astype(jnp.float32)).astype(jnp.bfloat16)
    return high, low


def dot(left, right):
    return jnp.dot(left, right, preferred_element_type=jnp.float32)


def product(parts, pair):
    width = pair.shape[1] // 2
    split = [halves(part) for part in parts]
    high = jnp.concatenate([one[0] for one in split], 1)
    low = jnp.concatenate([one[1] for one in split], 1)
    both = dot(high, pair[...])
    return both[:, :width] + both[:, width:] + dot(low, pair[:, :width])


def neighbours(field, start, rows, stride):
    return [field[pl.ds(start + shift, rows), :] for shift in (0, 1, -1, stride, -stride)]


def columns(row, lanes):
    return jnp.transpose(jnp.broadcast_to(row, (lanes, lanes)))


def pack_kernel(count, right_side, coef, first, second, turned):
    values = right_side.shape[1]
    depth = first.shape[0] - 8
    device = device_number()
    live = count[device]
    is_even = device % 2 == 0
    tail = pl.multiple_of(live - depth, 8)
    for out, start in (
        (first, jnp.where(is_even, tail, 0)),
        (second, jnp.where(is_even, 0, tail)),
    ):
        start = pl.multiple_of(start, 8)
        out[:depth, :] = right_side[pl.ds(start, depth), :]
        row = start // values
        lane = start % values
        turned[: coef.shape[0], :] = pltpu.roll(coef[...], (values - lane) % values, 1)
        lanes = lax.broadcasted_iota(jnp.int32, (8, values), 1)
        near = turned[pl.ds(row, 8), :]
        far = turned[pl.ds(row + 1, 8), :]
        out[depth:, :] = jnp.where(lanes < values - lane, near, far)


def prepare_kernel(
    cell_matrix, face_near, face_far, prolong, coef, coupling, restrict, spread, own_coef, own_jacobi, diag
):
    values = cell_matrix.shape[0]
    near = face_near[...]
    far = face_far[...]
    blocks = (cell_matrix[...], -near, -jnp.transpose(near), -far, -jnp.transpose(far))
    for index, block in enumerate(blocks):
        rows = pl.ds(index * values, values)
        high, low = halves(block)
        coupling[rows, :values] = high
        coupling[rows, values:] = low
    for child in range(CHILDREN):
        rows = pl.ds(child * values, values)
        block = prolong[child]
        high, low = halves(block)
        spread[:values, rows] = high
        spread[values:, rows] = low
        high, low = halves(jnp.transpose(block))
        restrict[rows, :values] = high
        restrict[rows, values:] = low
    row_index = lax.broadcasted_iota(jnp.int32, (values, values), 0)
    lane_index = lax.broadcasted_iota(jnp.int32, (values, values), 1)
    diagonal = jnp.sum(
        jnp.where(row_index == lane_index, cell_matrix[...], 0.0), axis=0, keepdims=True
    )
    diag[...] = jnp.broadcast_to(diagonal, diag.shape)
    for row in range(coef.shape[0]):
        rows = pl.ds(row * values, values)
        column = columns(coef[row : row + 1, :], values)
        own_coef[rows, :] = column
        own_jacobi[rows, :] = 1.0 / (column + diagonal)


def fine_kernel(
    count, right_side, first, second, coupling, restrict, own_coef, own_jacobi, diag,
    iterate, residual, coef, jacobi, message, update, coarse_coef,
):
    capacity, values = right_side.shape
    stride = capacity // 16
    depth = first.shape[0] - 8
    frame = capacity + 2 * depth
    device = device_number()
    total = device_total()
    live = count[device]
    is_even = device % 2 == 0
    end = pl.multiple_of(depth + live, 8)
    left = jnp.where(is_even, second[...], first[...])
    right = jnp.where(is_even, first[...], second[...])
    diagonal = diag[0:1, :]

    def column_of(side):
        pieces = []
        for row in range(-(-depth // values)):
            pieces.append(columns(side[depth + row : depth + row + 1, :], values))
        return jnp.concatenate(pieces, 0)[:depth]

    left_coef = column_of(left)
    right_coef = column_of(right)
    residual[:depth, :] = left[:depth]
    residual[pl.ds(depth, capacity), :] = right_side[...]
    residual[pl.ds(depth + capacity, depth), :] = jnp.zeros((depth, values), jnp.float32)
    residual[pl.ds(end, depth), :] = right[:depth]
    coef[:depth, :] = left_coef
    coef[pl.ds(depth, capacity), :] = own_coef[...]
    coef[pl.ds(depth + capacity, depth), :] = jnp.zeros((depth, values), jnp.float32)
    coef[pl.ds(end, depth), :] = right_coef
    jacobi[:depth, :] = jnp.where(device > 0, 1.0 / (left_coef + diagonal), 0.0)
    jacobi[pl.ds(depth, capacity), :] = own_jacobi[...]
    jacobi[pl.ds(depth + capacity, depth), :] = jnp.zeros((depth, values), jnp.float32)
    jacobi[pl.ds(end, depth), :] = jnp.where(device < total - 1, 1.0 / (right_coef + diagonal), 0.0)
    update[...] = jnp.zeros(update.shape, jnp.float32)
    iterate[...] = jnp.zeros(iterate.shape, jnp.float32)

    def step(index, carry):
        keep, gain = step_weights(index)
        fresh = keep * update[...] + gain * (jacobi[...] * residual[...])
        update[...] = fresh
        iterate[...] += fresh
        span = (frame - 2 * stride) // 2
        for block in range(2):
            start = stride + block * span
            rows = pl.ds(start, span)
            applied = product(neighbours(update, start, span, stride), coupling)
            residual[rows, :] = residual[rows, :] - (coef[rows, :] * update[rows, :] + applied)
        return carry

    lax.fori_loop(0, DEG, step, 0)
    cells = message.shape[0] - 8
    first_row = depth - CHILDREN * ((cells - capacity // CHILDREN) // 2)
    parts = [residual[pl.ds(first_row + c, cells, stride=CHILDREN), :] for c in range(CHILDREN)]
    message[:cells, :] = product(parts, restrict)
    mean = coef[pl.ds(first_row, cells, stride=CHILDREN), :]
    for c in range(1, CHILDREN):
        mean = mean + coef[pl.ds(first_row + c, cells, stride=CHILDREN), :]
    coarse_coef[...] = jnp.zeros(coarse_coef.shape, jnp.float32)
    coarse_coef[:cells, :] = mean * (1.0 / CHILDREN)
    message[cells:, :] = jnp.transpose(coarse_coef[...])[:8]


def coarse_kernel(
    count, iterate, residual, coef, jacobi, own, before_one, before_two, after_one, after_two,
    coupling, spread, diag, out, solved, source, coarse_coef, coarse_jacobi, coarse_update, coarse, update,
):
    capacity, values = out.shape
    stride = capacity // 16
    slots = capacity // CHILDREN
    margin = (own.shape[0] - 8 - slots) // 2
    depth = (iterate.shape[0] - capacity) // 2
    reach = depth // 2 // CHILDREN
    base = 2 * slots + margin
    device = device_number()
    total = device_total()

    def cells_of(offset):
        at = device + offset
        inside = (at >= 0) & (at < total)
        return jnp.where(inside, count[jnp.clip(at, 0, total - 1)] // CHILDREN, 0)

    size = cells_of(0)
    start_before = base - cells_of(-1)
    start_after = base + size
    start_last = start_after + cells_of(1)
    source[...] = jnp.zeros(source.shape, jnp.float32)
    coarse_coef[...] = jnp.zeros(coarse_coef.shape, jnp.float32)
    placed = (
        (before_two, start_before - cells_of(-2) - margin, 0, slots + 2 * margin),
        (before_one, start_before, margin, slots),
        (own, base, margin, slots),
        (after_one, start_after, margin, slots),
        (after_two, start_last, margin, slots + margin),
    )
    for piece, at, begin, rows in placed:
        source[pl.ds(at, rows), :] = piece[begin : begin + rows, :]
        column = columns(piece[slots + 2 * margin : slots + 2 * margin + 1, :], values)
        coarse_coef[pl.ds(at, rows), :] = column[begin : begin + rows]
    lowest = start_before - cells_of(-2) - jnp.where(device > 2, margin, 0)
    highest = start_last + cells_of(2) + jnp.where(device < total - 3, margin, 0)
    row_index = lax.broadcasted_iota(jnp.int32, source.shape, 0)
    inside = (row_index >= lowest) & (row_index < highest)
    coarse_jacobi[...] = jnp.where(inside, 1.0 / (coarse_coef[...] + diag[0:1, :]), 0.0)
    fresh = STEPS[0][1] * (coarse_jacobi[...] * source[...])
    coarse_update[...] = fresh
    coarse[...] = fresh
    low = base - slots - margin
    high = base + 2 * slots + margin
    for index in range(1, DEG):
        keep, gain = STEPS[index]
        rows = pl.ds(low, high - low)
        applied = product(neighbours(coarse_update, low, high - low, stride), coupling)
        source[rows, :] = source[rows, :] - (coarse_coef[rows, :] * coarse_update[rows, :] + applied)
        fresh = keep * coarse_update[rows, :] + gain * (coarse_jacobi[rows, :] * source[rows, :])
        coarse_update[rows, :] = fresh
        coarse[rows, :] += fresh
    count_rows = slots + 2 * reach
    correction = coarse[pl.ds(base - reach, count_rows), :]
    high_part, low_part = halves(correction)
    spread_high = spread[:values, :]
    children = dot(high_part, spread_high) + dot(low_part, spread_high) + dot(high_part, spread[values:, :])
    first_row = depth - CHILDREN * reach
    for c in range(CHILDREN):
        update[pl.ds(first_row + c, count_rows, stride=CHILDREN), :] = children[:, c * values : (c + 1) * values]
    used = pl.ds(first_row, CHILDREN * count_rows)
    solved[used, :] = iterate[used, :] + update[used, :]
    work = pl.ds(first_row, CHILDREN * count_rows)
    update[pl.ds(first_row - stride, stride), :] = jnp.zeros((stride, values), jnp.float32)
    update[pl.ds(first_row + CHILDREN * count_rows, stride), :] = jnp.zeros((stride, values), jnp.float32)
    solved_residual = residual

    def step(index, carry):
        keep, gain = step_weights(index)
        span = (CHILDREN * count_rows - 2 * stride) // 2
        for block in range(2):
            start = first_row + stride + block * span
            rows = pl.ds(start, span)
            applied = product(neighbours(update, start, span, stride), coupling)
            solved_residual[rows, :] = solved_residual[rows, :] - (coef[rows, :] * update[rows, :] + applied)
        fresh = keep * update[work, :] + gain * (jacobi[work, :] * solved_residual[work, :])
        update[work, :] = fresh
        solved[work, :] += fresh
        return carry

    lax.fori_loop(0, DEG, step, 0)
    live = count[device]
    is_live = lax.broadcasted_iota(jnp.int32, (capacity, values), 0) < live
    out[...] = jnp.where(is_live, solved[pl.ds(depth, capacity), :], 0.0)


def exchange(block, distance, phase):
    total = lax.axis_size(AXES)
    pairs = []
    for device in range(total - distance):
        if (device // distance) % 2 == phase:
            pairs += [(device, device + distance), (device + distance, device)]
    return lax.ppermute(block, AXES, pairs)


def shards(right_side, cell_coef, fine_count, cell_matrix, face_near, face_far, prolong):
    capacity, values = right_side.shape
    stride = capacity // 16
    depth = 6 * stride
    frame = capacity + 2 * depth
    slots = capacity // CHILDREN
    margin = 16
    coef_rows = jnp.concatenate(
        [cell_coef.reshape(capacity // values, values), jnp.ones((8 - capacity // values, values), jnp.float32)], 0
    )
    f32 = lambda *shape: jax.ShapeDtypeStruct(shape, jnp.float32)
    bf16 = lambda *shape: jax.ShapeDtypeStruct(shape, jnp.bfloat16)
    buffer = lambda *shape: pltpu.VMEM(shape, jnp.float32)
    smem = pl.BlockSpec(memory_space=pltpu.SMEM)
    vmem = pl.BlockSpec(memory_space=pltpu.VMEM)

    first, second = pl.pallas_call(
        pack_kernel,
        out_shape=(f32(depth + 8, values), f32(depth + 8, values)),
        in_specs=[smem, vmem, vmem],
        out_specs=(vmem, vmem),
        scratch_shapes=[buffer(24, values)],
        name="pack",
    )(fine_count, right_side, coef_rows)
    first_in = exchange(first, 1, 0)
    second_in = exchange(second, 1, 1)
    coupling, restrict, spread, own_coef, own_jacobi, diag = pl.pallas_call(
        prepare_kernel,
        out_shape=(
            bf16(5 * values, 2 * values),
            bf16(CHILDREN * values, 2 * values),
            bf16(2 * values, CHILDREN * values),
            f32(capacity, values),
            f32(capacity, values),
            f32(8, values),
        ),
        in_specs=[vmem] * 5,
        out_specs=(vmem,) * 6,
        name="prepare",
    )(cell_matrix, face_near, face_far, prolong, cell_coef.reshape(capacity // values, values))
    iterate, residual, coef, jacobi, message = pl.pallas_call(
        fine_kernel,
        out_shape=(f32(frame, values),) * 4 + (f32(slots + 2 * margin + 8, values),),
        in_specs=[smem] + [vmem] * 8,
        out_specs=(vmem,) * 5,
        scratch_shapes=[buffer(frame, values), buffer(values, values)],
        name="fine",
    )(fine_count, right_side, first_in, second_in, coupling, restrict, own_coef, own_jacobi, diag)
    one_a = exchange(message, 1, 0)
    one_b = exchange(message, 1, 1)
    two_a = exchange(message, 2, 0)
    two_b = exchange(message, 2, 1)
    device = device_number()
    is_even = device % 2 == 0
    is_low = device % 4 < 2
    before_one = jnp.where(is_even, one_b, one_a)
    after_one = jnp.where(is_even, one_a, one_b)
    before_two = jnp.where(is_low, two_b, two_a)
    after_two = jnp.where(is_low, two_a, two_b)
    coarse_frame = 5 * slots + 3 * margin
    return pl.pallas_call(
        coarse_kernel,
        out_shape=f32(capacity, values),
        in_specs=[smem] + [vmem] * 12,
        out_specs=vmem,
        scratch_shapes=[buffer(frame, values)] + [buffer(coarse_frame, values)] * 5 + [buffer(frame, values)],
        name="coarse",
    )(
        fine_count, iterate, residual, coef, jacobi, message, before_one, before_two, after_one, after_two,
        coupling, spread, diag,
    )


def solution(mesh):
    placed = (P(AXES, None), P(AXES), P(), P(), P(), P(), P())
    return jax.shard_map(
        shards, mesh=mesh, in_specs=placed, out_specs=P(AXES, None), check_vma=False
    )
```

time: 93 us -> 35.3 us (0.38)
  starting transfers between devices: 31.1 us -> 13 us
  Pallas kernels: 0 us -> 15 us
  between operations: 12.7 us -> 0.1 us
  matrix products: 12.4 us -> 0 us
  waiting for transfers between devices: 12.1 us -> 3.48 us
  local copies, waits for them, and re-layouts: 9.72 us -> 1.92 us
  blocking collectives: 7.35 us -> 0 us
  other arithmetic: 7.02 us -> 1.32 us
    ppermute x10 -> x6, starting transfers between devices: 31.1 us -> 13 us  [exchange(): return lax.ppermute(block, AXES, pairs)]
    pallas_call x0 -> x4, Pallas kernels: none -> 15 us  [the longest x1 5.61 us: shards(): pl.pallas_call(coarse_kernel, out_shape=f32(capacity, values), in_specs=[...]
    dot_general x10 -> x0, matrix products: 12.4 us -> none  [the longest x6 10.4 us: local_apply(): jnp.dot(joined, coupling, precision=lax.Precision.HIGHEST, preferred_elem...]
    ppermute x10 -> x6, waiting for transfers between devices: 12.1 us -> 3.48 us  [exchange(): return lax.ppermute(block, AXES, pairs)]
    unnamed x1 -> x0, blocking collectives: 3.92 us -> none
    all_gather x1 -> x0, blocking collectives: 3.43 us -> none  [shards(): lax.all_gather(coarse_source, 'lvl', axis=0, tiled=True)]
    select_n x5 -> x2, other arithmetic: 3.61 us -> 1.32 us  [the longest x1 0.68 us: shards(): after_one = jnp.where(is_even, one_a, one_b)]
    dynamic_update_slice x9 -> x0, local copies, waits for them, and re-layouts: 1.92 us -> none  [the longest x3 1.08 us: widen(): lax.dynamic_update_slice_in_dim(buffer, ghost_rows[3 * depth:], depth + l...]
  transfers between devices with their start and end apart: 10 -> 6, of which waited for: 3 -> 2; matrix products, arithmetic and copies ran while one was open for 10% -> 2% of each run, Pallas kernels for 0% -> 7%
where the time goes in v1:
time: 35.3 us; the launch traced here: 34.8 us
  Pallas kernels  15 us (42%)
  starting transfers between devices  13 us (37%)
  waiting for transfers between devices  3.48 us (10%)
  local copies, waits for them, and re-layouts  1.92 us (5%)
  other arithmetic  1.32 us (4%)
    ppermute x6, starting transfers between devices, exchange(): return lax.ppermute(block, AXES, pairs)  13 us
    pallas_call x1, Pallas kernels, shards(): pl.pallas_call(coarse_kernel, out_shape=f32(capacity, values), in_specs=[...  5.61 us
    pallas_call x1, Pallas kernels, shards(): pl.pallas_call(fine_kernel, out_shape=(f32(frame, values),) * 4 + (f32(sl...  5.09 us
    ppermute x6, waiting for transfers between devices, exchange(): return lax.ppermute(block, AXES, pairs)  3.48 us
    pallas_call x1, Pallas kernels, shards(): pl.pallas_call(prepare_kernel, out_shape=(bf16(5 * values, 2 * values), b...  2.58 us
    pallas_call x1, Pallas kernels, shards(): pl.pallas_call(pack_kernel, out_shape=(f32(depth + 8, values), f32(depth...  1.75 us
    concatenate x1, local copies, waits for them, and re-layouts, shards(): jnp.concatenate([cell_coef.reshape(capacity // values, values), jnp.ones(...  1.28 us
  transfers between devices with their start and end apart: 6, of which 2 were waited for; matrix products, arithmetic and copies ran while one was open for 2% of the time, Pallas kernels for 7%

profile of v1, /device:TPU:15, one launch (start us, length us, event | category | flops | bytes accessed | tf_op | source)
XLA Modules:
  0.0 34.8 jit_solution(379255668880727288)
XLA Ops:
  0.0 1.3 %concatenate.3.coef = f32[8,128]{1,0:T(8,128)} pad(f32[4,128]{1,0:T(4,128)} %bitcast.1, f32[]{:T(128)} %constant.26.clone.1), padding=0_4x0_0 | pad | bytes 6148 | tf_op jit(solution)/shard_map/concatenate | solution.py:299
  1.3 1.7 %pack.1 = (f32[200,128]{1,0:T(8,128)}, f32[200,128]{1,0:T(8,128)}) custom-call(s32[32]{0:T(128)} %count.5, f32[512,128]{1,0:T(8,128)} %right_side.3, f32[8,128]{1,0:T(8,128)} %concatenate.3.coef), custom_call_target="tpu_custom_call" | custom-call | tf_op jit(solution)/shard_map/pack/pallas_call | solution.py:308
  3.0 0.2 collective-permute-start
  3.3 5.0 %collective-permute-start.1 = (f32[200,128]{1,0:T(8,128)}, f32[200,128]{1,0:T(8,128)S(1)}, u32[]{:S(2)}, u32[]{:S(2)}) collective-permute-start(f32[200,128]{1,0:T(8,128)} %get-tuple-element.19), channel_id=1, source_target_pairs={{1,2},{2,1},{3,4},{4,3},{5,6},{6,5},{7,8},{8,7},{9,10},{10,9},{11,... | collective-permute-start | bytes 307208 | tf_op jit(solution)/shard_map/ppermute | solution.py:289
  8.2 2.6 %prepare.1 = (bf16[640,256]{1,0:T(8,128)(2,1)}, bf16[1024,256]{1,0:T(8,128)(2,1)}, bf16[256,1024]{1,0:T(8,128)(2,1)}, f32[512,128]{1,0:T(8,128)}, f32[512,128]{1,0:T(8,128)}, /*index=5*/f32[8,128]{1,0:T(8,128)}) custom-call(f32[128,128]{1,0:T(8,128)} %cell_matrix.1, f32[128,128]{1,0:T(8,128)} %face_near.1, f32[128,128]{1,0:T(8,128)} %face_far.1, ...), custom_call_target="tpu_custom_call" | custom-call | tf_op jit(solution)/shard_map/prepare/pallas_call | solution.py:318
  10.8 0.0 collective-permute-done.first
  10.8 0.0 copy-start
  10.8 0.4 %collective-permute-done.1.second = f32[200,128]{1,0:T(8,128)S(1)} collective-permute-done((f32[200,128]{1,0:T(8,128)}, f32[200,128]{1,0:T(8,128)S(1)}, u32[]{:S(2)}, u32[]{:S(2)}) %collective-permute-start.1) | collective-permute-done | bytes 102432 | tf_op jit(solution)/shard_map/ppermute | solution.py:289
  11.2 0.0 copy-start.1
  11.2 0.2 copy-done
  11.4 0.4 %copy-done.1 = f32[200,128]{1,0:T(8,128)} copy-done((f32[200,128]{1,0:T(8,128)}, f32[200,128]{1,0:T(8,128)S(1)}, u32[]{:S(2)}) %copy-start.1) | copy-done | bytes 102424
  11.9 5.1 %fine.1 = (f32[896,128]{1,0:T(8,128)}, f32[896,128]{1,0:T(8,128)}, f32[896,128]{1,0:T(8,128)}, f32[896,128]{1,0:T(8,128)}, f32[104,128]{1,0:T(8,128)}) custom-call(s32[32]{0:T(128)} %count.5, f32[512,128]{1,0:T(8,128)} %right_side.3, f32[200,128]{1,0:T(8,128)} %copy-done, f32[200,128]{1,0:T(8,128)} %copy-done.1, ...), custom_call_target="tpu_custom_call" | custom-call | tf_op jit(solution)/shard_map/fine/pallas_call | solution.py:332
  16.9 0.0 copy-start.2
  17.0 0.0 collective-permute-start.3
  17.0 5.1 %collective-permute-start.2 = (f32[104,128]{1,0:T(8,128)}, f32[104,128]{1,0:T(8,128)S(1)}, u32[]{:S(2)}, u32[]{:S(2)}) collective-permute-start(f32[104,128]{1,0:T(8,128)} %get-tuple-element.29.own), channel_id=1, source_target_pairs={{1,2},{2,1},{3,4},{4,3},{5,6},{6,5},{7,8},{8,7},{9,10},{10,9},{11,... | collective-permute-start | bytes 159752 | tf_op jit(solution)/shard_map/ppermute | solution.py:289
  22.1 0.0 copy-done.2
  22.1 0.1 collective-permute-start.5
  22.2 2.6 %collective-permute-start.4 = (f32[104,128]{1,0:T(8,128)S(1)}, f32[104,128]{1,0:T(8,128)S(1)}, u32[]{:S(2)}, u32[]{:S(2)}) collective-permute-start(f32[104,128]{1,0:T(8,128)S(1)} %copy-done.2), channel_id=1, source_target_pairs={{2,4},{4,2},{3,5},{5,3},{6,8},{8,6},{7,9},{9,7},{10,12},{12,10},{1... | collective-permute-start | bytes 159752 | tf_op jit(solution)/shard_map/ppermute | solution.py:289
  24.8 0.0 collective-permute-done.3
  24.8 0.0 collective-permute-done.2
  24.8 0.7 %broadcast_select_fusion.2 = (f32[104,128]{1,0:T(8,128)}, f32[104,128]{1,0:T(8,128)}) fusion(f32[104,128]{1,0:T(8,128)S(1)} %collective-permute-done.3, f32[104,128]{1,0:T(8,128)S(1)} %collective-permute-done.2, pred[]{:T(512)S(6)} %eq.6), kind=kLoop, calls=%fused_computation.2 | loop fusion | flops 26624 | bytes 212993 | tf_op jit(solution)/shard_map/jit(_where)/select_n | solution.py:348
  25.5 0.0 collective-permute-done.5
  25.5 3.1 %collective-permute-done.4 = f32[104,128]{1,0:T(8,128)S(1)} collective-permute-done((f32[104,128]{1,0:T(8,128)S(1)}, f32[104,128]{1,0:T(8,128)S(1)}, u32[]{:S(2)}, u32[]{:S(2)}) %collective-permute-start.4) | collective-permute-done | bytes 53280 | tf_op jit(solution)/shard_map/ppermute | solution.py:289
  28.5 0.6 %broadcast_select_fusion = (f32[104,128]{1,0:T(8,128)}, f32[104,128]{1,0:T(8,128)}) fusion(f32[104,128]{1,0:T(8,128)S(1)} %collective-permute-done.5, f32[104,128]{1,0:T(8,128)S(1)} %collective-permute-done.4, pred[]{:T(512)S(6)} %lt.15), kind=kLoop, calls=%fused_computation | loop fusion | flops 26624 | bytes 212993 | tf_op jit(solution)/shard_map/jit(_where)/select_n | solution.py:350
  29.2 5.6 %coarse.1 = f32[512,128]{1,0:T(8,128)} custom-call(s32[32]{0:T(128)} %count.5, f32[896,128]{1,0:T(8,128)} %get-tuple-element.25.iterate, f32[896,128]{1,0:T(8,128)} %get-tuple-element.26.residual, f32[896,128]{1,0:T(8,128)} %get-tuple-element.27.coef, f32[896,128]{1,0:T(8,128)} %get-tuple-element.28.jacobi, f32[104,128]{1,0:T(8,128)} %get-tuple-element.29.own, ...), custom_call_target="tpu_custom_call" | custom-call | tf_op jit(solution)/shard_map/coarse/pallas_call | solution.py:352
Async XLA Ops:
  3.0 7.8 %collective-permute-start = (f32[200,128]{1,0:T(8,128)}, f32[200,128]{1,0:T(8,128)S(1)}, u32[]{:S(2)}, u32[]{:S(2)}) collective-permute-start(f32[200,128]{1,0:T(8,128)} %get-tuple-element.18), channel_id=1, source_target_pairs={{0,1},{1,0},{2,3},{3,2},{4,5},{5,4},{6,7},{7,6},{8,9},{9,8},{10,11... | collective-permute-start | bytes 307208 | tf_op jit(solution)/shard_map/ppermute | solution.py:289
  3.3 8.0 %collective-permute-start.1 = (f32[200,128]{1,0:T(8,128)}, f32[200,128]{1,0:T(8,128)S(1)}, u32[]{:S(2)}, u32[]{:S(2)}) collective-permute-start(f32[200,128]{1,0:T(8,128)} %get-tuple-element.19), channel_id=1, source_target_pairs={{1,2},{2,1},{3,4},{4,3},{5,6},{6,5},{7,8},{8,7},{9,10},{10,9},{11,... | collective-permute-start | bytes 307208 | tf_op jit(solution)/shard_map/ppermute | solution.py:289
  10.8 0.6 %copy-start = (f32[200,128]{1,0:T(8,128)}, f32[200,128]{1,0:T(8,128)S(1)}, u32[]{:S(2)}) copy-start(f32[200,128]{1,0:T(8,128)S(1)} %collective-permute-done.first) | copy-start | bytes 307204
  11.2 0.6 %copy-start.1 = (f32[200,128]{1,0:T(8,128)}, f32[200,128]{1,0:T(8,128)S(1)}, u32[]{:S(2)}) copy-start(f32[200,128]{1,0:T(8,128)S(1)} %collective-permute-done.1.second) | copy-start | bytes 307204
  16.9 5.2 %copy-start.2 = (f32[104,128]{1,0:T(8,128)S(1)}, f32[104,128]{1,0:T(8,128)}, u32[]{:S(2)}) copy-start(f32[104,128]{1,0:T(8,128)} %get-tuple-element.29.own) | copy-start | bytes 159748
  17.0 7.8 %collective-permute-start.3 = (f32[104,128]{1,0:T(8,128)}, f32[104,128]{1,0:T(8,128)S(1)}, u32[]{:S(2)}, u32[]{:S(2)}) collective-permute-start(f32[104,128]{1,0:T(8,128)} %get-tuple-element.29.own), channel_id=1, source_target_pairs={{0,1},{1,0},{2,3},{3,2},{4,5},{5,4},{6,7},{7,6},{8,9},{9,8},{10,11... | collective-permute-start | bytes 159752 | tf_op jit(solution)/shard_map/ppermute | solution.py:289
  17.0 7.8 %collective-permute-start.2 = (f32[104,128]{1,0:T(8,128)}, f32[104,128]{1,0:T(8,128)S(1)}, u32[]{:S(2)}, u32[]{:S(2)}) collective-permute-start(f32[104,128]{1,0:T(8,128)} %get-tuple-element.29.own), channel_id=1, source_target_pairs={{1,2},{2,1},{3,4},{4,3},{5,6},{6,5},{7,8},{8,7},{9,10},{10,9},{11,... | collective-permute-start | bytes 159752 | tf_op jit(solution)/shard_map/ppermute | solution.py:289
  22.1 3.4 %collective-permute-start.5 = (f32[104,128]{1,0:T(8,128)S(1)}, f32[104,128]{1,0:T(8,128)S(1)}, u32[]{:S(2)}, u32[]{:S(2)}) collective-permute-start(f32[104,128]{1,0:T(8,128)S(1)} %copy-done.2), channel_id=1, source_target_pairs={{0,2},{2,0},{1,3},{3,1},{4,6},{6,4},{5,7},{7,5},{8,10},{10,8},{9,1... | collective-permute-start | bytes 159752 | tf_op jit(solution)/shard_map/ppermute | solution.py:289
  22.2 6.4 %collective-permute-start.4 = (f32[104,128]{1,0:T(8,128)S(1)}, f32[104,128]{1,0:T(8,128)S(1)}, u32[]{:S(2)}, u32[]{:S(2)}) collective-permute-start(f32[104,128]{1,0:T(8,128)S(1)} %copy-done.2), channel_id=1, source_target_pairs={{2,4},{4,2},{3,5},{5,3},{6,8},{8,6},{7,9},{9,7},{10,12},{12,10},{1... | collective-permute-start | bytes 159752 | tf_op jit(solution)/shard_map/ppermute | solution.py:289

commit v2 on v1

--- a/solution.py
+++ b/solution.py
@@ -10,6 +10,7 @@
 CENTER = 1.025
 RADIUS = 0.775
 CHILDREN = 8
+GRANT = 16 * 1024 * 1024
 
 
 def chebyshev_weights():
@@ -76,6 +77,8 @@
     device = device_number()
     live = count[device]
     is_even = device % 2 == 0
+    spare = jnp.ones((8 - coef.shape[0], values), jnp.float32)
+    rows_of_coef = jnp.concatenate([coef[...], spare], 0)
     tail = pl.multiple_of(live - depth, 8)
     for out, start in (
         (first, jnp.where(is_even, tail, 0)),
@@ -85,7 +88,7 @@
         out[:depth, :] = right_side[pl.ds(start, depth), :]
         row = start // values
         lane = start % values
-        turned[: coef.shape[0], :] = pltpu.roll(coef[...], (values - lane) % values, 1)
+        turned[:8, :] = pltpu.roll(rows_of_coef, (values - lane) % values, 1)
         lanes = lax.broadcasted_iota(jnp.int32, (8, values), 1)
         near = turned[pl.ds(row, 8), :]
         far = turned[pl.ds(row + 1, 8), :]
@@ -193,7 +196,7 @@
 
 
 def coarse_kernel(
-    count, iterate, residual, coef, jacobi, own, before_one, before_two, after_one, after_two,
+    count, iterate, residual, coef, jacobi, own, one_a, one_b, two_a, two_b,
     coupling, spread, diag, out, solved, source, coarse_coef, coarse_jacobi, coarse_update, coarse, update,
 ):
     capacity, values = out.shape
@@ -217,6 +220,12 @@
     start_last = start_after + cells_of(1)
     source[...] = jnp.zeros(source.shape, jnp.float32)
     coarse_coef[...] = jnp.zeros(coarse_coef.shape, jnp.float32)
+    is_even = device % 2 == 0
+    is_low = device % 4 < 2
+    before_one = jnp.where(is_even, one_b[...], one_a[...])
+    after_one = jnp.where(is_even, one_a[...], one_b[...])
+    before_two = jnp.where(is_low, two_b[...], two_a[...])
+    after_two = jnp.where(is_low, two_a[...], two_b[...])
     placed = (
         (before_two, start_before - cells_of(-2) - margin, 0, slots + 2 * margin),
         (before_one, start_before, margin, slots),
@@ -296,9 +305,7 @@
     frame = capacity + 2 * depth
     slots = capacity // CHILDREN
     margin = 16
-    coef_rows = jnp.concatenate(
-        [cell_coef.reshape(capacity // values, values), jnp.ones((8 - capacity // values, values), jnp.float32)], 0
-    )
+    coef_rows = cell_coef.reshape(capacity // values, values)
     f32 = lambda *shape: jax.ShapeDtypeStruct(shape, jnp.float32)
     bf16 = lambda *shape: jax.ShapeDtypeStruct(shape, jnp.bfloat16)
     buffer = lambda *shape: pltpu.VMEM(shape, jnp.float32)
@@ -312,9 +319,10 @@
         out_specs=(vmem, vmem),
         scratch_shapes=[buffer(24, values)],
         name="pack",
+        compiler_params=pltpu.CompilerParams(vmem_limit_bytes=GRANT),
     )(fine_count, right_side, coef_rows)
+    second_in = exchange(second, 1, 1)
     first_in = exchange(first, 1, 0)
-    second_in = exchange(second, 1, 1)
     coupling, restrict, spread, own_coef, own_jacobi, diag = pl.pallas_call(
         prepare_kernel,
         out_shape=(
@@ -328,7 +336,8 @@
         in_specs=[vmem] * 5,
         out_specs=(vmem,) * 6,
         name="prepare",
-    )(cell_matrix, face_near, face_far, prolong, cell_coef.reshape(capacity // values, values))
+        compiler_params=pltpu.CompilerParams(vmem_limit_bytes=GRANT),
+    )(cell_matrix, face_near, face_far, prolong, coef_rows)
     iterate, residual, coef, jacobi, message = pl.pallas_call(
         fine_kernel,
         out_shape=(f32(frame, values),) * 4 + (f32(slots + 2 * margin + 8, values),),
@@ -336,18 +345,12 @@
         out_specs=(vmem,) * 5,
         scratch_shapes=[buffer(frame, values), buffer(values, values)],
         name="fine",
+        compiler_params=pltpu.CompilerParams(vmem_limit_bytes=GRANT),
     )(fine_count, right_side, first_in, second_in, coupling, restrict, own_coef, own_jacobi, diag)
+    one_b = exchange(message, 1, 1)
+    two_b = exchange(message, 2, 1)
     one_a = exchange(message, 1, 0)
-    one_b = exchange(message, 1, 1)
     two_a = exchange(message, 2, 0)
-    two_b = exchange(message, 2, 1)
-    device = device_number()
-    is_even = device % 2 == 0
-    is_low = device % 4 < 2
-    before_one = jnp.where(is_even, one_b, one_a)
-    after_one = jnp.where(is_even, one_a, one_b)
-    before_two = jnp.where(is_low, two_b, two_a)
-    after_two = jnp.where(is_low, two_a, two_b)
     coarse_frame = 5 * slots + 3 * margin
     return pl.pallas_call(
         coarse_kernel,
@@ -356,8 +359,9 @@
         out_specs=vmem,
         scratch_shapes=[buffer(frame, values)] + [buffer(coarse_frame, values)] * 5 + [buffer(frame, values)],
         name="coarse",
+        compiler_params=pltpu.CompilerParams(vmem_limit_bytes=GRANT),
     )(
-        fine_count, iterate, residual, coef, jacobi, message, before_one, before_two, after_one, after_two,
+        fine_count, iterate, residual, coef, jacobi, message, one_a, one_b, two_a, two_b,
         coupling, spread, diag,
     )
 

time: 35.3 us -> 31.9 us (0.904)
  the two profiles are of different devices: /device:TPU:15 before, /device:TPU:2 now
where the time goes in v2:
time: 31.9 us; the launch traced here: 31.6 us
  starting transfers between devices  11.8 us (37%)
  Pallas kernels  9.27 us (29%)
  waiting for transfers between devices  7.18 us (23%)
  local copies, waits for them, and re-layouts  3.34 us (10%)
    ppermute x6, starting transfers between devices, exchange(): return lax.ppermute(block, AXES, pairs)  11.8 us
    ppermute x6, waiting for transfers between devices, exchange(): return lax.ppermute(block, AXES, pairs)  7.18 us
    pallas_call x1, Pallas kernels, shards(): pl.pallas_call(coarse_kernel, out_shape=f32(capacity, values), in_specs=[...  4.64 us
    pallas_call x1, Pallas kernels, shards(): pl.pallas_call(fine_kernel, out_shape=(f32(frame, values),) * 4 + (f32(sl...  3.66 us
    unnamed x18, local copies, waits for them, and re-layouts  3.34 us
    pallas_call x1, Pallas kernels, shards(): pl.pallas_call(pack_kernel, out_shape=(f32(depth + 8, values), f32(depth...  0.65 us
  transfers between devices with their start and end apart: 6, of which 3 were waited for; matrix products, arithmetic and copies ran while one was open for 0% of the time, Pallas kernels for 1%

profile of v2, /device:TPU:2, one launch (start us, length us, event | category | flops | bytes accessed | tf_op | source)
XLA Modules:
  0.0 31.6 jit_solution(15633432767481983095)
XLA Ops:
  0.0 0.0 copy-start.8
  0.0 0.7 %copy-done.8 = s32[32]{0:T(128)S(1)} copy-done((s32[32]{0:T(128)S(1)}, s32[32]{0:T(128)}, u32[]{:S(2)}) %copy-start.8) | copy-done | bytes 152
  0.7 0.0 copy-start
  0.7 0.9 %copy-done = f32[512,128]{1,0:T(8,128)S(1)} copy-done((f32[512,128]{1,0:T(8,128)S(1)}, f32[512,128]{1,0:T(8,128)}, u32[]{:S(2)}) %copy-start) | copy-done | bytes 262168
  1.6 0.0 copy-start.6
  1.6 0.7 %copy-done.6 = f32[512]{0:T(512)S(1)} copy-done((f32[512]{0:T(512)S(1)}, f32[512]{0:T(512)}, u32[]{:S(2)}) %copy-start.6) | copy-done | bytes 2072
  2.3 0.0 copy-start.3
  2.3 0.0 copy-start.4
  2.3 0.0 copy-start.5
  2.3 0.7 %pack.1 = (f32[200,128]{1,0:T(8,128)S(1)}, f32[200,128]{1,0:T(8,128)S(1)}) custom-call(s32[32]{0:T(128)S(1)} %copy-done.8, f32[512,128]{1,0:T(8,128)S(1)} %copy-done, f32[4,128]{1,0:T(4,128)S(1)} %bitcast.1), custom_call_target="tpu_custom_call" | custom-call | tf_op jit(solution)/shard_map/pack/pallas_call | solution.py:315
  2.9 0.0 copy-start.7
  2.9 1.6 %collective-permute-start = (f32[200,128]{1,0:T(8,128)S(1)}, f32[200,128]{1,0:T(8,128)S(1)}, u32[]{:S(2)}, u32[]{:S(2)}) collective-permute-start(f32[200,128]{1,0:T(8,128)S(1)} %get-tuple-element.18), channel_id=1, source_target_pairs={{0,1},{1,0},{2,3},{3,2},{4,5},{5,4},{6,7},{7,6},{8,9},{9,8},{10,11... | collective-permute-start | bytes 307208 | tf_op jit(solution)/shard_map/ppermute | solution.py:298
  4.5 0.0 copy-start.1
  4.5 2.0 %collective-permute-start.1 = (f32[200,128]{1,0:T(8,128)S(1)}, f32[200,128]{1,0:T(8,128)S(1)}, u32[]{:S(2)}, u32[]{:S(2)}) collective-permute-start(f32[200,128]{1,0:T(8,128)S(1)} %get-tuple-element.19), channel_id=1, source_target_pairs={{1,2},{2,1},{3,4},{4,3},{5,6},{6,5},{7,8},{8,7},{9,10},{10,9},{11,... | collective-permute-start | bytes 307208 | tf_op jit(solution)/shard_map/ppermute | solution.py:298
  6.5 0.0 copy-done.3
  6.6 0.0 copy-done.4
  6.6 0.0 copy-done.5
  6.6 0.0 copy-done.7
  6.6 0.0 copy-start.2
  6.6 1.0 %copy-done.2 = f32[8,128,128]{2,1,0:T(8,128)S(1)} copy-done((f32[8,128,128]{2,1,0:T(8,128)S(1)}, f32[8,128,128]{2,1,0:T(8,128)}, u32[]{:S(2)}) %copy-start.2) | copy-done | bytes 524312
  7.6 0.3 %prepare.1 = (bf16[640,256]{1,0:T(8,128)(2,1)S(1)}, bf16[1024,256]{1,0:T(8,128)(2,1)S(1)}, bf16[256,1024]{1,0:T(8,128)(2,1)S(1)}, f32[512,128]{1,0:T(8,128)S(1)}...) custom-call(f32[128,128]{1,0:T(8,128)S(1)} %copy-done.3, f32[128,128]{1,0:T(8,128)S(1)} %copy-done.4, ...), custom_call_target="tpu_custom_call" | custom-call | tf_op jit(solution)/shard_map/prepare/pallas_call | solution.py:326
  8.0 0.0 collective-permute-done.first
  8.0 3.5 %collective-permute-done.1.second = f32[200,128]{1,0:T(8,128)S(1)} collective-permute-done((f32[200,128]{1,0:T(8,128)S(1)}, f32[200,128]{1,0:T(8,128)S(1)}, u32[]{:S(2)}, u32[]{:S(2)}) %collective-permute-start.1) | collective-permute-done | bytes 102432 | tf_op jit(solution)/shard_map/ppermute | solution.py:298
  11.5 0.0 copy-done.1
  11.5 3.7 %fine.1 = (f32[896,128]{1,0:T(8,128)S(1)}, f32[896,128]{1,0:T(8,128)S(1)}, f32[896,128]{1,0:T(8,128)S(1)}, f32[896,128]{1,0:T(8,128)S(1)}, f32[104,128]{1,0:T(8,128)S(1)}) custom-call(s32[32]{0:T(128)S(1)} %copy-done.8, f32[512,128]{1,0:T(8,128)S(1)} %copy-done.1, f32[200,128]{1,0:T(8,128)S(1)} %collective-permute-done.first, ...), custom_call_target="tpu_custom_call" | custom-call | tf_op jit(solution)/shard_map/fine/pallas_call | solution.py:341
  15.2 1.9 %collective-permute-start.5 = (f32[104,128]{1,0:T(8,128)S(1)}, f32[104,128]{1,0:T(8,128)S(1)}, u32[]{:S(2)}, u32[]{:S(2)}) collective-permute-start(f32[104,128]{1,0:T(8,128)S(1)} %get-tuple-element.29.own), channel_id=1, source_target_pairs={{2,4},{4,2},{3,5},{5,3},{6,8},{8,6},{7,9},{9,7},{10,12},{12,10},{1... | collective-permute-start | bytes 159752 | tf_op jit(solution)/shard_map/ppermute | solution.py:298
  17.1 2.6 %collective-permute-start.4 = (f32[104,128]{1,0:T(8,128)S(1)}, f32[104,128]{1,0:T(8,128)S(1)}, u32[]{:S(2)}, u32[]{:S(2)}) collective-permute-start(f32[104,128]{1,0:T(8,128)S(1)} %get-tuple-element.29.own), channel_id=1, source_target_pairs={{0,2},{2,0},{1,3},{3,1},{4,6},{6,4},{5,7},{7,5},{8,10},{10,8},{9,1... | collective-permute-start | bytes 159752 | tf_op jit(solution)/shard_map/ppermute | solution.py:298
  19.7 1.9 %collective-permute-start.3 = (f32[104,128]{1,0:T(8,128)S(1)}, f32[104,128]{1,0:T(8,128)S(1)}, u32[]{:S(2)}, u32[]{:S(2)}) collective-permute-start(f32[104,128]{1,0:T(8,128)S(1)} %get-tuple-element.29.own), channel_id=1, source_target_pairs={{1,2},{2,1},{3,4},{4,3},{5,6},{6,5},{7,8},{8,7},{9,10},{10,9},{11,... | collective-permute-start | bytes 159752 | tf_op jit(solution)/shard_map/ppermute | solution.py:298
  21.6 1.7 %collective-permute-start.2 = (f32[104,128]{1,0:T(8,128)S(1)}, f32[104,128]{1,0:T(8,128)S(1)}, u32[]{:S(2)}, u32[]{:S(2)}) collective-permute-start(f32[104,128]{1,0:T(8,128)S(1)} %get-tuple-element.29.own), channel_id=1, source_target_pairs={{0,1},{1,0},{2,3},{3,2},{4,5},{5,4},{6,7},{7,6},{8,9},{9,8},{10,11... | collective-permute-start | bytes 159752 | tf_op jit(solution)/shard_map/ppermute | solution.py:298
  23.3 0.0 collective-permute-done.5.two_b
  23.3 0.0 collective-permute-done.4.two_a
  23.4 2.8 %collective-permute-done.3.one_b = f32[104,128]{1,0:T(8,128)S(1)} collective-permute-done((f32[104,128]{1,0:T(8,128)S(1)}, f32[104,128]{1,0:T(8,128)S(1)}, u32[]{:S(2)}, u32[]{:S(2)}) %collective-permute-start.3) | collective-permute-done | bytes 53280 | tf_op jit(solution)/shard_map/ppermute | solution.py:298
  26.2 0.8 %collective-permute-done.2.one_a = f32[104,128]{1,0:T(8,128)S(1)} collective-permute-done((f32[104,128]{1,0:T(8,128)S(1)}, f32[104,128]{1,0:T(8,128)S(1)}, u32[]{:S(2)}, u32[]{:S(2)}) %collective-permute-start.2) | collective-permute-done | bytes 53280 | tf_op jit(solution)/shard_map/ppermute | solution.py:298
  27.0 4.6 %coarse.1 = f32[512,128]{1,0:T(8,128)} custom-call(s32[32]{0:T(128)S(1)} %copy-done.8, f32[896,128]{1,0:T(8,128)S(1)} %get-tuple-element.25.iterate, f32[896,128]{1,0:T(8,128)S(1)} %get-tuple-element.26.residual, f32[896,128]{1,0:T(8,128)S(1)} %get-tuple-element.27.coef, f32[896,128]{1,0:T(8,128)S(1)} %get-tuple-element.28.jacobi, ...), custom_call_target="tpu_custom_call" | custom-call | tf_op jit(solution)/shard_map/coarse/pallas_call | solution.py:355
Async XLA Ops:
  0.0 0.7 %copy-start.8 = (s32[32]{0:T(128)S(1)}, s32[32]{0:T(128)}, u32[]{:S(2)}) copy-start(s32[32]{0:T(128)} %count.5) | copy-start | bytes 388
  0.7 0.9 %copy-start = (f32[512,128]{1,0:T(8,128)S(1)}, f32[512,128]{1,0:T(8,128)}, u32[]{:S(2)}) copy-start(f32[512,128]{1,0:T(8,128)} %right_side.3) | copy-start | bytes 786436
  1.6 0.7 %copy-start.6 = (f32[512]{0:T(512)S(1)}, f32[512]{0:T(512)}, u32[]{:S(2)}) copy-start(f32[512]{0:T(512)} %param.8) | copy-start | bytes 6148
  2.3 4.3 %copy-start.3 = (f32[128,128]{1,0:T(8,128)S(1)}, f32[128,128]{1,0:T(8,128)}, u32[]{:S(2)}) copy-start(f32[128,128]{1,0:T(8,128)} %cell_matrix.1) | copy-start | bytes 196612
  2.3 4.3 %copy-start.4 = (f32[128,128]{1,0:T(8,128)S(1)}, f32[128,128]{1,0:T(8,128)}, u32[]{:S(2)}) copy-start(f32[128,128]{1,0:T(8,128)} %face_near.1) | copy-start | bytes 196612
  2.3 4.3 %copy-start.5 = (f32[128,128]{1,0:T(8,128)S(1)}, f32[128,128]{1,0:T(8,128)}, u32[]{:S(2)}) copy-start(f32[128,128]{1,0:T(8,128)} %face_far.1) | copy-start | bytes 196612
  2.9 3.6 %copy-start.7 = (f32[512]{0:T(512)S(1)}, f32[512]{0:T(512)}, u32[]{:S(2)}) copy-start(f32[512]{0:T(512)} %param.8) | copy-start | bytes 6148
  2.9 5.0 %collective-permute-start = (f32[200,128]{1,0:T(8,128)S(1)}, f32[200,128]{1,0:T(8,128)S(1)}, u32[]{:S(2)}, u32[]{:S(2)}) collective-permute-start(f32[200,128]{1,0:T(8,128)S(1)} %get-tuple-element.18), channel_id=1, source_target_pairs={{0,1},{1,0},{2,3},{3,2},{4,5},{5,4},{6,7},{7,6},{8,9},{9,8},{10,11... | collective-permute-start | bytes 307208 | tf_op jit(solution)/shard_map/ppermute | solution.py:298
  4.5 7.0 %copy-start.1 = (f32[512,128]{1,0:T(8,128)S(1)}, f32[512,128]{1,0:T(8,128)}, u32[]{:S(2)}) copy-start(f32[512,128]{1,0:T(8,128)} %right_side.3) | copy-start | bytes 786436
  4.5 7.0 %collective-permute-start.1 = (f32[200,128]{1,0:T(8,128)S(1)}, f32[200,128]{1,0:T(8,128)S(1)}, u32[]{:S(2)}, u32[]{:S(2)}) collective-permute-start(f32[200,128]{1,0:T(8,128)S(1)} %get-tuple-element.19), channel_id=1, source_target_pairs={{1,2},{2,1},{3,4},{4,3},{5,6},{6,5},{7,8},{8,7},{9,10},{10,9},{11,... | collective-permute-start | bytes 307208 | tf_op jit(solution)/shard_map/ppermute | solution.py:298
  6.6 1.0 %copy-start.2 = (f32[8,128,128]{2,1,0:T(8,128)S(1)}, f32[8,128,128]{2,1,0:T(8,128)}, u32[]{:S(2)}) copy-start(f32[8,128,128]{2,1,0:T(8,128)} %prolong.1) | copy-start | bytes 1572868
  15.2 8.2 %collective-permute-start.5 = (f32[104,128]{1,0:T(8,128)S(1)}, f32[104,128]{1,0:T(8,128)S(1)}, u32[]{:S(2)}, u32[]{:S(2)}) collective-permute-start(f32[104,128]{1,0:T(8,128)S(1)} %get-tuple-element.29.own), channel_id=1, source_target_pairs={{2,4},{4,2},{3,5},{5,3},{6,8},{8,6},{7,9},{9,7},{10,12},{12,10},{1... | collective-permute-start | bytes 159752 | tf_op jit(solution)/shard_map/ppermute | solution.py:298
  17.1 6.3 %collective-permute-start.4 = (f32[104,128]{1,0:T(8,128)S(1)}, f32[104,128]{1,0:T(8,128)S(1)}, u32[]{:S(2)}, u32[]{:S(2)}) collective-permute-start(f32[104,128]{1,0:T(8,128)S(1)} %get-tuple-element.29.own), channel_id=1, source_target_pairs={{0,2},{2,0},{1,3},{3,1},{4,6},{6,4},{5,7},{7,5},{8,10},{10,8},{9,1... | collective-permute-start | bytes 159752 | tf_op jit(solution)/shard_map/ppermute | solution.py:298
  19.7 6.4 %collective-permute-start.3 = (f32[104,128]{1,0:T(8,128)S(1)}, f32[104,128]{1,0:T(8,128)S(1)}, u32[]{:S(2)}, u32[]{:S(2)}) collective-permute-start(f32[104,128]{1,0:T(8,128)S(1)} %get-tuple-element.29.own), channel_id=1, source_target_pairs={{1,2},{2,1},{3,4},{4,3},{5,6},{6,5},{7,8},{8,7},{9,10},{10,9},{11,... | collective-permute-start | bytes 159752 | tf_op jit(solution)/shard_map/ppermute | solution.py:298
  21.6 5.4 %collective-permute-start.2 = (f32[104,128]{1,0:T(8,128)S(1)}, f32[104,128]{1,0:T(8,128)S(1)}, u32[]{:S(2)}, u32[]{:S(2)}) collective-permute-start(f32[104,128]{1,0:T(8,128)S(1)} %get-tuple-element.29.own), channel_id=1, source_target_pairs={{0,1},{1,0},{2,3},{3,2},{4,5},{5,4},{6,7},{7,6},{8,9},{9,8},{10,11... | collective-permute-start | bytes 159752 | tf_op jit(solution)/shard_map/ppermute | solution.py:298

commit v3 on v2

v3 whole, which is shorter than its diff:
```python
import jax
import jax.numpy as jnp
from jax import lax
from jax.experimental import pallas as pl
from jax.experimental.pallas import tpu as pltpu
from jax.sharding import PartitionSpec as P

DEG = 3
AXES = ("sfc", "lvl")
CENTER = 1.025
RADIUS = 0.775
CHILDREN = 8
NEAR_CELLS = 2
GRANT = 16 * 1024 * 1024


def chebyshev_weights():
    sigma = CENTER / RADIUS
    weight = 1.0 / sigma
    steps = [(0.0, 1.0 / CENTER)]
    for _ in range(DEG - 1):
        following = 1.0 / (2.0 * sigma - weight)
        steps.append((following * weight, 2.0 * following / RADIUS))
        weight = following
    return steps


STEPS = chebyshev_weights()


def device_number():
    return lax.axis_index("sfc") * lax.axis_size("lvl") + lax.axis_index("lvl")


def device_total():
    return lax.axis_size("sfc") * lax.axis_size("lvl")


def halves(value):
    high = value.astype(jnp.bfloat16)
    low = (value - high.astype(jnp.float32)).astype(jnp.bfloat16)
    return high, low


def dot(left, right):
    return jnp.dot(left, right, preferred_element_type=jnp.float32)


def product(parts, pair):
    width = pair.shape[1] // 2
    split = [halves(part) for part in parts]
    high = jnp.concatenate([one[0] for one in split], 1)
    low = jnp.concatenate([one[1] for one in split], 1)
    both = dot(high, pair[...])
    return both[:, :width] + both[:, width:] + dot(low, pair[:, :width])


def neighbours(field, start, rows, stride):
    return [field[pl.ds(start + shift, rows), :] for shift in (0, 1, -1, stride, -stride)]


def columns(row, lanes):
    return jnp.transpose(jnp.broadcast_to(row, (lanes, lanes)))


def scalar_of(numbers, index):
    return numbers[index : index + 1, 0:1][0, 0]


def pack_kernel(count_in, right_in, coef_in, first, second, numbers, count, right_side, coef, turned, arrivals):
    values = right_side.shape[1]
    depth = first.shape[0] - 8
    copies = (
        pltpu.make_async_copy(count_in, count, arrivals.at[0]),
        pltpu.make_async_copy(right_in, right_side, arrivals.at[1]),
        pltpu.make_async_copy(coef_in, coef.at[pl.ds(0, coef_in.shape[0])], arrivals.at[2]),
    )
    for copy in copies:
        copy.start()
    device = device_number()
    total = device_total()
    coef[pl.ds(coef_in.shape[0], 8 - coef_in.shape[0]), :] = jnp.ones(
        (8 - coef_in.shape[0], values), jnp.float32
    )
    turned[...] = jnp.ones(turned.shape, jnp.float32)
    copies[0].wait()
    rows = lax.broadcasted_iota(jnp.int32, numbers.shape, 0)
    table = jnp.zeros(numbers.shape, jnp.int32)
    for offset in range(-NEAR_CELLS, NEAR_CELLS + 1):
        at = device + offset
        size = jnp.where((at >= 0) & (at < total), count[jnp.clip(at, 0, total - 1)], 0)
        table = jnp.where(rows == offset + NEAR_CELLS, size, table)
    numbers[...] = table
    live = count[device]
    is_even = device % 2 == 0
    tail = live - depth
    copies[2].wait()
    for out, start in (
        (first, jnp.where(is_even, tail, 0)),
        (second, jnp.where(is_even, 0, tail)),
    ):
        row = start // values
        lane = start % values
        turned[:8, :] = pltpu.roll(coef[...], (values - lane) % values, 1)
        lanes = lax.broadcasted_iota(jnp.int32, (8, values), 1)
        near = turned[pl.ds(row, 8), :]
        far = turned[pl.ds(row + 1, 8), :]
        out[depth:, :] = jnp.where(lanes < values - lane, near, far)
    copies[1].wait()
    for out, start in (
        (first, jnp.where(is_even, tail, 0)),
        (second, jnp.where(is_even, 0, tail)),
    ):
        out[:depth, :] = right_side[pl.ds(pl.multiple_of(start, 8), depth), :]


def interior_kernel(
    numbers, right_in, coef_in, cell_in, near_in, far_in, prolong_in,
    coupling, restrict, spread, diag, residual, coef, jacobi, *rest,
):
    updates = rest[:DEG]
    coef_rows, cell_matrix, face_near, face_far, prolong, arrivals = rest[DEG:]
    values = cell_in.shape[0]
    capacity = right_in.shape[0]
    stride = capacity // 16
    depth = (residual.shape[0] - capacity) // 2
    right_side = residual.at[pl.ds(depth, capacity)]
    copies = [
        pltpu.make_async_copy(origin, target, arrivals.at[index])
        for index, (origin, target) in enumerate(
            (
                (cell_in, cell_matrix),
                (near_in, face_near),
                (far_in, face_far),
                (coef_in, coef_rows),
                (right_in, right_side),
                (prolong_in, prolong),
            )
        )
    ]
    for copy in copies:
        copy.start()
    spare = pl.ds(depth + capacity, depth)
    for field in (residual, coef, jacobi) + updates:
        field[spare, :] = jnp.zeros((depth, values), jnp.float32)
    for copy in copies[:5]:
        copy.wait()
    near = face_near[...]
    far = face_far[...]
    blocks = (cell_matrix[...], -near, -jnp.transpose(near), -far, -jnp.transpose(far))
    for index, block in enumerate(blocks):
        rows = pl.ds(index * values, values)
        high, low = halves(block)
        coupling[rows, :values] = high
        coupling[rows, values:] = low
    row_index = lax.broadcasted_iota(jnp.int32, (values, values), 0)
    lane_index = lax.broadcasted_iota(jnp.int32, (values, values), 1)
    diagonal = jnp.sum(
        jnp.where(row_index == lane_index, cell_matrix[...], 0.0), axis=0, keepdims=True
    )
    diag[...] = jnp.broadcast_to(diagonal, diag.shape)
    keep, gain = STEPS[0]
    for row in range(capacity // values):
        rows = pl.ds(depth + row * values, values)
        column = columns(coef_rows[row : row + 1, :], values)
        source = residual[rows, :]
        scale = 1.0 / (column + diagonal)
        coef[rows, :] = column
        jacobi[rows, :] = scale
        updates[0][rows, :] = gain * (scale * source)
    end = depth + scalar_of(numbers, NEAR_CELLS)
    for index in range(1, DEG + 1):
        start = depth + index * stride
        span = capacity - 2 * index * stride
        rows = pl.ds(start, span)
        before = updates[index - 1]
        old = residual[rows, :]
        fresh = old - (
            coef[rows, :] * before[rows, :] + product(neighbours(before, start, span, stride), coupling)
        )
        inside = start + lax.broadcasted_iota(jnp.int32, (span, values), 0) < end - index * stride
        residual[rows, :] = jnp.where(inside, fresh, old)
        if index < DEG:
            keep, gain = STEPS[index]
            updates[index][rows, :] = keep * before[rows, :] + gain * (jacobi[rows, :] * fresh)
    copies[5].wait()
    for child in range(CHILDREN):
        rows = pl.ds(child * values, values)
        block = prolong[child]
        high, low = halves(block)
        spread[:values, rows] = high
        spread[values:, rows] = low
        high, low = halves(jnp.transpose(block))
        restrict[rows, :values] = high
        restrict[rows, values:] = low


def boundary_kernel(
    numbers, first, second, coupling, restrict, diag, *fields
):
    residual, coef, jacobi = fields[DEG + 3 : DEG + 6]
    updates = fields[DEG + 6 : 2 * DEG + 6]
    message, coarse_coef = fields[2 * DEG + 6 :]
    frame, values = residual.shape
    depth = first.shape[0] - 8
    capacity = frame - 2 * depth
    stride = capacity // 16
    device = device_number()
    total = device_total()
    is_even = device % 2 == 0
    end = pl.multiple_of(depth + scalar_of(numbers, NEAR_CELLS), 8)
    diagonal = diag[0:1, :]
    left = jnp.where(is_even, second[...], first[...])
    right = jnp.where(is_even, first[...], second[...])
    keep, gain = STEPS[0]
    for side, start, exists in ((left, 0, device > 0), (right, end, device < total - 1)):
        pieces = []
        for row in range(-(-depth // values)):
            pieces.append(columns(side[depth + row : depth + row + 1, :], values))
        column = jnp.concatenate(pieces, 0)[:depth]
        scale = jnp.where(exists, 1.0 / (column + diagonal), 0.0)
        rows = pl.ds(start, depth)
        residual[rows, :] = side[:depth]
        coef[rows, :] = column
        jacobi[rows, :] = scale
        updates[0][rows, :] = gain * (scale * side[:depth])
    for index in range(1, DEG + 1):
        before = updates[index - 1]
        starts = (index * stride, pl.multiple_of(end - index * stride, 8))
        parts = [
            jnp.concatenate([before[pl.ds(start + shift, depth), :] for start in starts], 0)
            for shift in (0, 1, -1, stride, -stride)
        ]
        applied = product(parts, coupling)
        for side, start in enumerate(starts):
            rows = pl.ds(start, depth)
            own = parts[0][side * depth : (side + 1) * depth]
            fresh = residual[rows, :] - (coef[rows, :] * own + applied[side * depth : (side + 1) * depth])
            residual[rows, :] = fresh
            if index < DEG:
                keep, gain = STEPS[index]
                updates[index][rows, :] = keep * own + gain * (jacobi[rows, :] * fresh)
    cells = message.shape[0] - 8
    first_row = depth - CHILDREN * ((cells - capacity // CHILDREN) // 2)
    parts = [residual[pl.ds(first_row + c, cells, stride=CHILDREN), :] for c in range(CHILDREN)]
    message[:cells, :] = product(parts, restrict)
    mean = coef[pl.ds(first_row, cells, stride=CHILDREN), :]
    for c in range(1, CHILDREN):
        mean = mean + coef[pl.ds(first_row + c, cells, stride=CHILDREN), :]
    coarse_coef[...] = jnp.zeros(coarse_coef.shape, jnp.float32)
    coarse_coef[:cells, :] = mean * (1.0 / CHILDREN)
    message[cells:, :] = jnp.transpose(coarse_coef[...])[:8]


def coarse_kernel(
    numbers, residual, coef, jacobi, *rest
):
    presmoothed = rest[:DEG]
    own, one_a, one_b, two_a, two_b, coupling, spread, diag, out_hbm = rest[DEG : DEG + 9]
    source, coarse_coef, coarse_jacobi = rest[DEG + 9 : DEG + 12]
    coarse_updates = rest[DEG + 12 : 2 * DEG + 12]
    updates = rest[2 * DEG + 12 : 3 * DEG + 12]
    out, sent = rest[3 * DEG + 12 :]
    capacity, values = out.shape
    stride = capacity // 16
    slots = capacity // CHILDREN
    margin = (own.shape[0] - 8 - slots) // 2
    depth = (residual.shape[0] - capacity) // 2
    reach = depth // 2 // CHILDREN
    base = 2 * slots + margin
    device = device_number()
    total = device_total()

    def cells_of(offset):
        return scalar_of(numbers, NEAR_CELLS + offset) // CHILDREN

    start_before = base - cells_of(-1)
    start_first = start_before - cells_of(-2)
    start_after = base + cells_of(0)
    start_last = start_after + cells_of(1)
    source[...] = jnp.zeros(source.shape, jnp.float32)
    coarse_coef[...] = jnp.zeros(coarse_coef.shape, jnp.float32)
    is_even = device % 2 == 0
    is_low = device % 4 < 2
    before_one = jnp.where(is_even, one_b[...], one_a[...])
    after_one = jnp.where(is_even, one_a[...], one_b[...])
    before_two = jnp.where(is_low, two_b[...], two_a[...])
    after_two = jnp.where(is_low, two_a[...], two_b[...])
    placed = (
        (before_two, start_first - margin, 0, slots + 2 * margin),
        (before_one, start_before, margin, slots),
        (own, base, margin, slots),
        (after_one, start_after, margin, slots),
        (after_two, start_last, margin, slots + margin),
    )
    for piece, at, begin, rows in placed:
        source[pl.ds(at, rows), :] = piece[begin : begin + rows, :]
        column = columns(piece[slots + 2 * margin : slots + 2 * margin + 1, :], values)
        coarse_coef[pl.ds(at, rows), :] = column[begin : begin + rows]
    lowest = start_first - jnp.where(device > 2, margin, 0)
    highest = start_last + cells_of(2) + jnp.where(device < total - 3, margin, 0)
    row_index = lax.broadcasted_iota(jnp.int32, source.shape, 0)
    inside = (row_index >= lowest) & (row_index < highest)
    coarse_jacobi[...] = jnp.where(inside, 1.0 / (coarse_coef[...] + diag[0:1, :]), 0.0)
    coarse_updates[0][...] = STEPS[0][1] * (coarse_jacobi[...] * source[...])
    for index in range(1, DEG):
        keep, gain = STEPS[index]
        before = coarse_updates[index - 1]
        start = base - margin - (DEG - 1 - index) * stride
        span = slots + 2 * margin + 2 * (DEG - 1 - index) * stride
        rows = pl.ds(start, span)
        own_update = before[rows, :]
        fresh = source[rows, :] - (
            coarse_coef[rows, :] * own_update + product(neighbours(before, start, span, stride), coupling)
        )
        source[rows, :] = fresh
        coarse_updates[index][rows, :] = keep * own_update + gain * (coarse_jacobi[rows, :] * fresh)
    count_rows = slots + 2 * reach
    rows = pl.ds(base - reach, count_rows)
    correction = coarse_updates[0][rows, :]
    for index in range(1, DEG):
        correction = correction + coarse_updates[index][rows, :]
    high_part, low_part = halves(correction)
    spread_high = spread[:values, :]
    children = dot(high_part, spread_high) + dot(low_part, spread_high) + dot(high_part, spread[values:, :])
    first_row = depth - CHILDREN * reach
    for c in range(CHILDREN):
        updates[0][pl.ds(first_row + c, count_rows, stride=CHILDREN), :] = children[:, c * values : (c + 1) * values]
    for index in range(DEG):
        keep, gain = STEPS[index]
        before = updates[index]
        begin = first_row + (index + 1) * stride
        span = (CHILDREN * count_rows - 2 * (index + 1) * stride) // 2
        for block in range(2):
            start = begin + block * span
            rows = pl.ds(start, span)
            own_update = before[rows, :]
            fresh = residual[rows, :] - (
                coef[rows, :] * own_update + product(neighbours(before, start, span, stride), coupling)
            )
            step = gain * (jacobi[rows, :] * fresh)
            if index > 0:
                step = step + keep * own_update
            if index < DEG - 1:
                residual[rows, :] = fresh
                updates[index + 1][rows, :] = step
            else:
                total_update = step
                for field in presmoothed + updates:
                    total_update = total_update + field[rows, :]
                slot = start - depth
                is_live = slot + lax.broadcasted_iota(jnp.int32, (span, values), 0) < scalar_of(numbers, NEAR_CELLS)
                out[pl.ds(slot, span), :] = jnp.where(is_live, total_update, 0.0)
                pltpu.make_async_copy(
                    out.at[pl.ds(slot, span)], out_hbm.at[pl.ds(slot, span)], sent.at[block]
                ).start()
    for block in range(2):
        piece = pl.ds(block * (capacity // 2), capacity // 2)
        pltpu.make_async_copy(out.at[piece], out_hbm.at[piece], sent.at[block]).wait()


def exchange(block, distance, phase, complete):
    total = lax.axis_size(AXES)
    pairs = []
    for device in range(total - distance):
        if (device // distance) % 2 == phase:
            pairs += [(device, device + distance), (device + distance, device)]
    if complete:
        busy = {source for source, _ in pairs}
        idle = [device for device in range(total) if device not in busy]
        for one, other in zip(idle[0::2], idle[1::2]):
            pairs += [(one, other), (other, one)]
    return lax.ppermute(block, AXES, pairs)


def shards(right_side, cell_coef, fine_count, cell_matrix, face_near, face_far, prolong):
    capacity, values = right_side.shape
    stride = capacity // 16
    depth = 2 * DEG * stride
    frame = capacity + 2 * depth
    slots = capacity // CHILDREN
    margin = 16
    coef_rows = cell_coef.reshape(capacity // values, values)
    f32 = lambda *shape: jax.ShapeDtypeStruct(shape, jnp.float32)
    bf16 = lambda *shape: jax.ShapeDtypeStruct(shape, jnp.bfloat16)
    buffer = lambda *shape: pltpu.VMEM(shape, jnp.float32)
    vmem = pl.BlockSpec(memory_space=pltpu.VMEM)
    hbm = pl.BlockSpec(memory_space=pltpu.HBM)
    params = pltpu.CompilerParams(vmem_limit_bytes=GRANT)
    off_chip = lambda array: pltpu.with_memory_space_constraint(array, pltpu.HBM)

    first, second, numbers = pl.pallas_call(
        pack_kernel,
        out_shape=(
            f32(depth + 8, values),
            f32(depth + 8, values),
            jax.ShapeDtypeStruct((8, values), jnp.int32),
        ),
        in_specs=[hbm, hbm, hbm],
        out_specs=(vmem, vmem, vmem),
        scratch_shapes=[
            pltpu.SMEM(fine_count.shape, jnp.int32),
            buffer(capacity, values),
            buffer(8, values),
            buffer(24, values),
            pltpu.SemaphoreType.DMA((3,)),
        ],
        name="pack",
        compiler_params=params,
    )(off_chip(fine_count), off_chip(right_side), off_chip(coef_rows))
    second_in = exchange(second, 1, 1, True)
    first_in = exchange(first, 1, 0, False)
    prepared = pl.pallas_call(
        interior_kernel,
        out_shape=(
            bf16(5 * values, 2 * values),
            bf16(CHILDREN * values, 2 * values),
            bf16(2 * values, CHILDREN * values),
            f32(8, values),
        )
        + (f32(frame, values),) * (3 + DEG),
        in_specs=[vmem] + [hbm] * 6,
        out_specs=(vmem,) * (7 + DEG),
        scratch_shapes=[
            buffer(*coef_rows.shape),
            buffer(values, values),
            buffer(values, values),
            buffer(values, values),
            buffer(*prolong.shape),
            pltpu.SemaphoreType.DMA((6,)),
        ],
        name="interior",
        compiler_params=params,
    )(numbers, *(off_chip(each) for each in (right_side, coef_rows, cell_matrix, face_near, face_far, prolong)))
    coupling, restrict, spread, diag = prepared[:4]
    *fields, message = pl.pallas_call(
        boundary_kernel,
        out_shape=(f32(frame, values),) * (3 + DEG) + (f32(slots + 2 * margin + 8, values),),
        in_specs=[vmem] * (9 + DEG),
        out_specs=(vmem,) * (4 + DEG),
        scratch_shapes=[buffer(values, values)],
        input_output_aliases={6 + index: index for index in range(3 + DEG)},
        name="boundary",
        compiler_params=params,
    )(numbers, first_in, second_in, coupling, restrict, diag, *prepared[4:])
    one_b = exchange(message, 1, 1, False)
    two_b = exchange(message, 2, 1, True)
    one_a = exchange(message, 1, 0, False)
    two_a = exchange(message, 2, 0, False)
    coarse_frame = 5 * slots + 3 * margin
    return pl.pallas_call(
        coarse_kernel,
        out_shape=f32(capacity, values),
        in_specs=[vmem] * (4 + DEG + 8),
        out_specs=hbm,
        scratch_shapes=[buffer(coarse_frame, values)] * (3 + DEG)
        + [buffer(frame, values)] * DEG
        + [buffer(capacity, values), pltpu.SemaphoreType.DMA((2,))],
        name="coarse",
        compiler_params=params,
    )(numbers, *fields, message, one_a, one_b, two_a, two_b, coupling, spread, diag)


def solution(mesh):
    placed = (P(AXES, None), P(AXES), P(), P(), P(), P(), P())
    return jax.shard_map(
        shards, mesh=mesh, in_specs=placed, out_specs=P(AXES, None), check_vma=False
    )
```

time: 31.9 us -> 24.1 us (0.76)
  the two profiles are of different devices: /device:TPU:2 before, /device:TPU:0 now
where the time goes in v3:
time: 24.1 us; the launch traced here: 23.9 us
  starting transfers between devices  10.9 us (45%)
  Pallas kernels  8.98 us (37%)
  waiting for transfers between devices  3.93 us (16%)
    ppermute x6, starting transfers between devices, exchange(): return lax.ppermute(block, AXES, pairs)  10.9 us
    ppermute x6, waiting for transfers between devices, exchange(): return lax.ppermute(block, AXES, pairs)  3.93 us
    pallas_call x1, Pallas kernels, shards(): pl.pallas_call(coarse_kernel, out_shape=f32(capacity, values), in_specs=[...  3.4 us
    pallas_call x1, Pallas kernels, shards(): pl.pallas_call(interior_kernel, out_shape=(bf16(5 * values, 2 * values),...  2.76 us
    pallas_call x1, Pallas kernels, shards(): pl.pallas_call(boundary_kernel, out_shape=(f32(frame, values),) * (3 + DE...  1.83 us
    pallas_call x1, Pallas kernels, shards(): pl.pallas_call(pack_kernel, out_shape=(f32(depth + 8, values), f32(depth...  0.99 us
  transfers between devices with their start and end apart: 6, of which 2 were waited for; matrix products, arithmetic and copies ran while one was open for 0% of the time, Pallas kernels for 12%

profile of v3, /device:TPU:0, one launch (start us, length us, event | category | flops | bytes accessed | tf_op | source)
XLA Modules:
  0.0 23.9 jit_solution(10676240374790918089)
XLA Ops:
  0.0 1.0 %pack.1 = (f32[200,128]{1,0:T(8,128)S(1)}, f32[200,128]{1,0:T(8,128)S(1)}, s32[8,128]{1,0:T(8,128)S(1)}) custom-call(s32[32]{0:T(128)} %count_in.1, f32[512,128]{1,0:T(8,128)} %right_in.3, f32[4,128]{1,0:T(4,128)} %bitcast.1), custom_call_target="tpu_custom_call" | custom-call | tf_op jit(solution)/shard_map/pack/pallas_call | solution.py:392
  1.0 3.1 %collective-permute-start = (f32[200,128]{1,0:T(8,128)S(1)}, f32[200,128]{1,0:T(8,128)S(1)}, u32[]{:S(2)}, u32[]{:S(2)}) collective-permute-start(f32[200,128]{1,0:T(8,128)S(1)} %get-tuple-element.26), channel_id=1, source_target_pairs={{0,1},{1,0},{2,3},{3,2},{4,5},{5,4},{6,7},{7,6},{8,9},{9,8},{10,11... | collective-permute-start | bytes 307208 | tf_op jit(solution)/shard_map/ppermute | solution.py:373
  4.1 3.6 %collective-permute-start.1 = (f32[200,128]{1,0:T(8,128)S(1)}, f32[200,128]{1,0:T(8,128)S(1)}, u32[]{:S(2)}, u32[]{:S(2)}) collective-permute-start(f32[200,128]{1,0:T(8,128)S(1)} %get-tuple-element.27), channel_id=1, source_target_pairs={{1,2},{2,1},{3,4},{4,3},{5,6},{6,5},{7,8},{8,7},{9,10},{10,9},{11,... | collective-permute-start | bytes 307208 | tf_op jit(solution)/shard_map/ppermute | solution.py:373
  7.7 2.8 %interior.1 = (bf16[640,256]{1,0:T(8,128)(2,1)S(1)}, bf16[1024,256]{1,0:T(8,128)(2,1)S(1)}, bf16[256,1024]{1,0:T(8,128)(2,1)S(1)}, f32[8,128]{1,0:T(8,128)S(1)},...) custom-call(s32[8,128]{1,0:T(8,128)S(1)} %get-tuple-element.25.numbe, ...), custom_call_target="tpu_custom_call" | custom-call | tf_op jit(solution)/shard_map/interior/pallas_call | solution.py:413
  10.5 0.0 collective-permute-done.first
  10.5 1.3 %collective-permute-done.1.second = f32[200,128]{1,0:T(8,128)S(1)} collective-permute-done((f32[200,128]{1,0:T(8,128)S(1)}, f32[200,128]{1,0:T(8,128)S(1)}, u32[]{:S(2)}, u32[]{:S(2)}) %collective-permute-start.1) | collective-permute-done | bytes 102432 | tf_op jit(solution)/shard_map/ppermute | solution.py:373
  11.7 1.8 %boundary.1 = (f32[896,128]{1,0:T(8,128)S(1)}, f32[896,128]{1,0:T(8,128)S(1)}, f32[896,128]{1,0:T(8,128)S(1)}, f32[896,128]{1,0:T(8,128)S(1)}, f32[896,128]{1,0:...) custom-call(s32[8,128]{1,0:T(8,128)S(1)} %get-tuple-element.25.numbe, ...), custom_call_target="tpu_custom_call", output_to_operand_aliasing={{0}: (6, {}), {1}: (7, {}), {2}: (8, {}), {3}: (9, {}), {4}... | custom-call | tf_op jit(solution)/shard_map/boundary/pallas_call | solution.py:436
  13.6 0.1 collective-permute-start.5
  13.7 0.1 collective-permute-start.4
  13.7 0.7 %collective-permute-start.3 = (f32[104,128]{1,0:T(8,128)S(1)}, f32[104,128]{1,0:T(8,128)S(1)}, u32[]{:S(2)}, u32[]{:S(2)}) collective-permute-start(f32[104,128]{1,0:T(8,128)S(1)} %get-tuple-element.43.rest_3_), channel_id=1, source_target_pairs={{1,2},{2,1},{3,4},{4,3},{5,6},{6,5},{7,8},{8,7},{9,10},{10,9},{11,... | collective-permute-start | bytes 159752 | tf_op jit(solution)/shard_map/ppermute | solution.py:373
  14.4 3.4 %collective-permute-start.2 = (f32[104,128]{1,0:T(8,128)S(1)}, f32[104,128]{1,0:T(8,128)S(1)}, u32[]{:S(2)}, u32[]{:S(2)}) collective-permute-start(f32[104,128]{1,0:T(8,128)S(1)} %get-tuple-element.43.rest_3_), channel_id=1, source_target_pairs={{0,1},{1,0},{2,3},{3,2},{4,5},{5,4},{6,7},{7,6},{8,9},{9,8},{10,11... | collective-permute-start | bytes 159752 | tf_op jit(solution)/shard_map/ppermute | solution.py:373
  17.8 0.0 collective-permute-done.5.rest_7_
  17.8 0.0 collective-permute-done.4.rest_6_
  17.8 0.0 collective-permute-done.3.rest_5_
  17.8 2.6 %collective-permute-done.2.rest_4_ = f32[104,128]{1,0:T(8,128)S(1)} collective-permute-done((f32[104,128]{1,0:T(8,128)S(1)}, f32[104,128]{1,0:T(8,128)S(1)}, u32[]{:S(2)}, u32[]{:S(2)}) %collective-permute-start.2) | collective-permute-done | bytes 53280 | tf_op jit(solution)/shard_map/ppermute | solution.py:373
  20.5 3.4 %coarse.1 = f32[512,128]{1,0:T(8,128)} custom-call(s32[8,128]{1,0:T(8,128)S(1)} %get-tuple-element.25.numbers, f32[896,128]{1,0:T(8,128)S(1)} %get-tuple-element.37.residual, f32[896,128]{1,0:T(8,128)S(1)} %get-tuple-element.38.coef, f32[896,128]{1,0:T(8,128)S(1)} %get-tuple-element.39.jacobi, f32[896,128]{1,0:T(8,128)S(1)} %get-tuple-element.40.rest_0_, ...), custom_call_target="tpu_custom_call" | custom-call | tf_op jit(solution)/shard_map/coarse/pallas_call | solution.py:451
Async XLA Ops:
  1.0 9.5 %collective-permute-start = (f32[200,128]{1,0:T(8,128)S(1)}, f32[200,128]{1,0:T(8,128)S(1)}, u32[]{:S(2)}, u32[]{:S(2)}) collective-permute-start(f32[200,128]{1,0:T(8,128)S(1)} %get-tuple-element.26), channel_id=1, source_target_pairs={{0,1},{1,0},{2,3},{3,2},{4,5},{5,4},{6,7},{7,6},{8,9},{9,8},{10,11... | collective-permute-start | bytes 307208 | tf_op jit(solution)/shard_map/ppermute | solution.py:373
  4.1 7.7 %collective-permute-start.1 = (f32[200,128]{1,0:T(8,128)S(1)}, f32[200,128]{1,0:T(8,128)S(1)}, u32[]{:S(2)}, u32[]{:S(2)}) collective-permute-start(f32[200,128]{1,0:T(8,128)S(1)} %get-tuple-element.27), channel_id=1, source_target_pairs={{1,2},{2,1},{3,4},{4,3},{5,6},{6,5},{7,8},{8,7},{9,10},{10,9},{11,... | collective-permute-start | bytes 307208 | tf_op jit(solution)/shard_map/ppermute | solution.py:373
  13.6 4.3 %collective-permute-start.5 = (f32[104,128]{1,0:T(8,128)S(1)}, f32[104,128]{1,0:T(8,128)S(1)}, u32[]{:S(2)}, u32[]{:S(2)}) collective-permute-start(f32[104,128]{1,0:T(8,128)S(1)} %get-tuple-element.43.rest_3_), channel_id=1, source_target_pairs={{2,4},{4,2},{3,5},{5,3},{6,8},{8,6},{7,9},{9,7},{10,12},{12,10},{1... | collective-permute-start | bytes 159752 | tf_op jit(solution)/shard_map/ppermute | solution.py:373
  13.7 4.2 %collective-permute-start.4 = (f32[104,128]{1,0:T(8,128)S(1)}, f32[104,128]{1,0:T(8,128)S(1)}, u32[]{:S(2)}, u32[]{:S(2)}) collective-permute-start(f32[104,128]{1,0:T(8,128)S(1)} %get-tuple-element.43.rest_3_), channel_id=1, source_target_pairs={{0,2},{2,0},{1,3},{3,1},{4,6},{6,4},{5,7},{7,5},{8,10},{10,8},{9,1... | collective-permute-start | bytes 159752 | tf_op jit(solution)/shard_map/ppermute | solution.py:373
  13.7 4.1 %collective-permute-start.3 = (f32[104,128]{1,0:T(8,128)S(1)}, f32[104,128]{1,0:T(8,128)S(1)}, u32[]{:S(2)}, u32[]{:S(2)}) collective-permute-start(f32[104,128]{1,0:T(8,128)S(1)} %get-tuple-element.43.rest_3_), channel_id=1, source_target_pairs={{1,2},{2,1},{3,4},{4,3},{5,6},{6,5},{7,8},{8,7},{9,10},{10,9},{11,... | collective-permute-start | bytes 159752 | tf_op jit(solution)/shard_map/ppermute | solution.py:373
  14.4 6.1 %collective-permute-start.2 = (f32[104,128]{1,0:T(8,128)S(1)}, f32[104,128]{1,0:T(8,128)S(1)}, u32[]{:S(2)}, u32[]{:S(2)}) collective-permute-start(f32[104,128]{1,0:T(8,128)S(1)} %get-tuple-element.43.rest_3_), channel_id=1, source_target_pairs={{0,1},{1,0},{2,3},{3,2},{4,5},{5,4},{6,7},{7,6},{8,9},{9,8},{10,11... | collective-permute-start | bytes 159752 | tf_op jit(solution)/shard_map/ppermute | solution.py:373

commit v4 on v3

--- a/solution.py
+++ b/solution.py
@@ -36,6 +36,10 @@
     return lax.axis_size("sfc") * lax.axis_size("lvl")
 
 
+def is_near_end(device, total):
+    return (device == 1) | (device == 2) | (device == total - 3) | (device == total - 2)
+
+
 def halves(value):
     high = value.astype(jnp.bfloat16)
     low = (value - high.astype(jnp.float32)).astype(jnp.bfloat16)
@@ -48,15 +52,22 @@
 
 def product(parts, pair):
     width = pair.shape[1] // 2
+    odd = len(parts) % 2
     split = [halves(part) for part in parts]
-    high = jnp.concatenate([one[0] for one in split], 1)
-    low = jnp.concatenate([one[1] for one in split], 1)
+    high = jnp.concatenate([one[0] for one in split] + [split[-1][1]] * odd, 1)
+    low = jnp.concatenate([one[1] for one in split[: len(parts) - odd]], 1)
     both = dot(high, pair[...])
-    return both[:, :width] + both[:, width:] + dot(low, pair[:, :width])
+    return both[:, :width] + both[:, width:] + dot(low, pair[: low.shape[1], :width])
 
 
 def neighbours(field, start, rows, stride):
     return [field[pl.ds(start + shift, rows), :] for shift in (0, 1, -1, stride, -stride)]
+
+
+def far_rows(capacity):
+    stride = capacity // 16
+    slots = capacity // CHILDREN
+    return 2 * stride + DEG * stride // CHILDREN - slots // 2
 
 
 def columns(row, lanes):
@@ -147,7 +158,8 @@
         copy.wait()
     near = face_near[...]
     far = face_far[...]
-    blocks = (cell_matrix[...], -near, -jnp.transpose(near), -far, -jnp.transpose(far))
+    last = -jnp.transpose(far)
+    blocks = (cell_matrix[...], -near, -jnp.transpose(near), -far, last, last)
     for index, block in enumerate(blocks):
         rows = pl.ds(index * values, values)
         high, low = halves(block)
@@ -200,7 +212,7 @@
 ):
     residual, coef, jacobi = fields[DEG + 3 : DEG + 6]
     updates = fields[DEG + 6 : 2 * DEG + 6]
-    message, coarse_coef = fields[2 * DEG + 6 :]
+    message, far_even, far_odd, coarse, coarse_coef = fields[2 * DEG + 6 :]
     frame, values = residual.shape
     depth = first.shape[0] - 8
     capacity = frame - 2 * depth
@@ -240,34 +252,47 @@
             if index < DEG:
                 keep, gain = STEPS[index]
                 updates[index][rows, :] = keep * own + gain * (jacobi[rows, :] * fresh)
-    cells = message.shape[0] - 8
-    first_row = depth - CHILDREN * ((cells - capacity // CHILDREN) // 2)
+    cells = coarse.shape[0]
+    slots = capacity // CHILDREN
+    margin = (cells - slots) // 2
+    first_row = depth - CHILDREN * margin
     parts = [residual[pl.ds(first_row + c, cells, stride=CHILDREN), :] for c in range(CHILDREN)]
-    message[:cells, :] = product(parts, restrict)
+    source = product(parts, restrict)
+    coarse[...] = source
     mean = coef[pl.ds(first_row, cells, stride=CHILDREN), :]
     for c in range(1, CHILDREN):
         mean = mean + coef[pl.ds(first_row + c, cells, stride=CHILDREN), :]
     coarse_coef[...] = jnp.zeros(coarse_coef.shape, jnp.float32)
     coarse_coef[:cells, :] = mean * (1.0 / CHILDREN)
-    message[cells:, :] = jnp.transpose(coarse_coef[...])[:8]
+    lanes = jnp.transpose(coarse_coef[...])[:8]
+    message[:slots, :] = source[margin : margin + slots]
+    message[slots:, :] = pltpu.roll(lanes, values - margin, 1)
+    count = far_even.shape[0] - 8
+    near = far_rows(capacity)
+    tail = margin + scalar_of(numbers, NEAR_CELLS) // CHILDREN - near
+    is_low = device % 4 < 2
+    for out, start in ((far_even, jnp.where(is_low, tail, margin)), (far_odd, jnp.where(is_low, margin, tail))):
+        out[:count, :] = coarse[pl.ds(start, count), :]
+        out[count:, :] = pltpu.roll(lanes, values - start, 1)
 
 
 def coarse_kernel(
     numbers, residual, coef, jacobi, *rest
 ):
     presmoothed = rest[:DEG]
-    own, one_a, one_b, two_a, two_b, coupling, spread, diag, out_hbm = rest[DEG : DEG + 9]
-    source, coarse_coef, coarse_jacobi = rest[DEG + 9 : DEG + 12]
-    coarse_updates = rest[DEG + 12 : 2 * DEG + 12]
-    updates = rest[2 * DEG + 12 : 3 * DEG + 12]
-    out, sent = rest[3 * DEG + 12 :]
+    own, one_a, one_b, one_c, two_a, two_b, coupling, spread, diag, out_hbm = rest[DEG : DEG + 10]
+    source, coarse_coef, coarse_jacobi = rest[DEG + 10 : DEG + 13]
+    coarse_updates = rest[DEG + 13 : 2 * DEG + 13]
+    updates = rest[2 * DEG + 13 : 3 * DEG + 13]
+    out, sent = rest[3 * DEG + 13 :]
     capacity, values = out.shape
     stride = capacity // 16
     slots = capacity // CHILDREN
-    margin = (own.shape[0] - 8 - slots) // 2
+    near = far_rows(capacity)
+    margin = 16
     depth = (residual.shape[0] - capacity) // 2
     reach = depth // 2 // CHILDREN
-    base = 2 * slots + margin
+    base = slots + 3 * margin
     device = device_number()
     total = device_total()
 
@@ -275,30 +300,32 @@
         return scalar_of(numbers, NEAR_CELLS + offset) // CHILDREN
 
     start_before = base - cells_of(-1)
-    start_first = start_before - cells_of(-2)
     start_after = base + cells_of(0)
     start_last = start_after + cells_of(1)
     source[...] = jnp.zeros(source.shape, jnp.float32)
     coarse_coef[...] = jnp.zeros(coarse_coef.shape, jnp.float32)
     is_even = device % 2 == 0
     is_low = device % 4 < 2
-    before_one = jnp.where(is_even, one_b[...], one_a[...])
-    after_one = jnp.where(is_even, one_a[...], one_b[...])
+    one_odd = jnp.where(is_near_end(device, total), one_c[...], one_b[...])
+    before_one = jnp.where(is_even, one_odd, one_a[...])
+    after_one = jnp.where(is_even, one_a[...], one_odd)
     before_two = jnp.where(is_low, two_b[...], two_a[...])
     after_two = jnp.where(is_low, two_a[...], two_b[...])
     placed = (
-        (before_two, start_first - margin, 0, slots + 2 * margin),
-        (before_one, start_before, margin, slots),
-        (own, base, margin, slots),
-        (after_one, start_after, margin, slots),
-        (after_two, start_last, margin, slots + margin),
+        (before_two, start_before - near),
+        (before_one, start_before),
+        (own, base),
+        (after_one, start_after),
+        (after_two, start_last),
     )
-    for piece, at, begin, rows in placed:
-        source[pl.ds(at, rows), :] = piece[begin : begin + rows, :]
-        column = columns(piece[slots + 2 * margin : slots + 2 * margin + 1, :], values)
-        coarse_coef[pl.ds(at, rows), :] = column[begin : begin + rows]
-    lowest = start_first - jnp.where(device > 2, margin, 0)
-    highest = start_last + cells_of(2) + jnp.where(device < total - 3, margin, 0)
+    for piece, at in placed:
+        rows = piece.shape[0] - 8
+        source[pl.ds(at, rows), :] = piece[:rows, :]
+        coarse_coef[pl.ds(at, rows), :] = columns(piece[rows : rows + 1, :], values)[:rows]
+    beyond = cells_of(-2) + jnp.where(device > 2, margin, 0)
+    lowest = start_before - jnp.minimum(beyond, near)
+    beyond = cells_of(2) + jnp.where(device < total - 3, margin, 0)
+    highest = start_last + jnp.minimum(beyond, near)
     row_index = lax.broadcasted_iota(jnp.int32, source.shape, 0)
     inside = (row_index >= lowest) & (row_index < highest)
     coarse_jacobi[...] = jnp.where(inside, 1.0 / (coarse_coef[...] + diag[0:1, :]), 0.0)
@@ -370,6 +397,10 @@
         idle = [device for device in range(total) if device not in busy]
         for one, other in zip(idle[0::2], idle[1::2]):
             pairs += [(one, other), (other, one)]
+    return move(block, pairs)
+
+
+def move(block, pairs):
     return lax.ppermute(block, AXES, pairs)
 
 
@@ -380,6 +411,7 @@
     frame = capacity + 2 * depth
     slots = capacity // CHILDREN
     margin = 16
+    far = -(-far_rows(capacity) // 8) * 8 + 8
     coef_rows = cell_coef.reshape(capacity // values, values)
     f32 = lambda *shape: jax.ShapeDtypeStruct(shape, jnp.float32)
     bf16 = lambda *shape: jax.ShapeDtypeStruct(shape, jnp.bfloat16)
@@ -413,7 +445,7 @@
     prepared = pl.pallas_call(
         interior_kernel,
         out_shape=(
-            bf16(5 * values, 2 * values),
+            bf16(6 * values, 2 * values),
             bf16(CHILDREN * values, 2 * values),
             bf16(2 * values, CHILDREN * values),
             f32(8, values),
@@ -433,32 +465,42 @@
         compiler_params=params,
     )(numbers, *(off_chip(each) for each in (right_side, coef_rows, cell_matrix, face_near, face_far, prolong)))
     coupling, restrict, spread, diag = prepared[:4]
-    *fields, message = pl.pallas_call(
+    *fields, message, far_even, far_odd = pl.pallas_call(
         boundary_kernel,
-        out_shape=(f32(frame, values),) * (3 + DEG) + (f32(slots + 2 * margin + 8, values),),
+        out_shape=(f32(frame, values),) * (3 + DEG)
+        + (f32(slots + 8, values), f32(far, values), f32(far, values)),
         in_specs=[vmem] * (9 + DEG),
-        out_specs=(vmem,) * (4 + DEG),
-        scratch_shapes=[buffer(values, values)],
+        out_specs=(vmem,) * (6 + DEG),
+        scratch_shapes=[buffer(slots + 2 * margin, values), buffer(values, values)],
         input_output_aliases={6 + index: index for index in range(3 + DEG)},
         name="boundary",
         compiler_params=params,
     )(numbers, first_in, second_in, coupling, restrict, diag, *prepared[4:])
-    one_b = exchange(message, 1, 1, False)
-    two_b = exchange(message, 2, 1, True)
+    total = lax.axis_size(AXES)
+    ring = [(0, 1), (1, 2), (2, 0), (total - 3, total - 2), (total - 2, total - 1), (total - 1, total - 3)]
+    for device in range(3, total - 3, 2):
+        ring += [(device, device + 1), (device + 1, device)]
+    one_b = move(message, ring)
+    ends = [(1, 2), (2, 1), (0, 3), (3, 0)]
+    ends += [(total - 1 - source, total - 1 - target) for source, target in ends]
+    for device in range(4, total - 4):
+        ends += [(device, device + 2 if device % 4 < 2 else device - 2)]
+    one_c = move(message, ends)
+    two_b = exchange(far_odd, 2, 1, True)
     one_a = exchange(message, 1, 0, False)
-    two_a = exchange(message, 2, 0, False)
-    coarse_frame = 5 * slots + 3 * margin
+    two_a = exchange(far_even, 2, 0, False)
+    coarse_frame = 4 * slots + 4 * margin
     return pl.pallas_call(
         coarse_kernel,
         out_shape=f32(capacity, values),
-        in_specs=[vmem] * (4 + DEG + 8),
+        in_specs=[vmem] * (4 + DEG + 9),
         out_specs=hbm,
         scratch_shapes=[buffer(coarse_frame, values)] * (3 + DEG)
         + [buffer(frame, values)] * DEG
         + [buffer(capacity, values), pltpu.SemaphoreType.DMA((2,))],
         name="coarse",
         compiler_params=params,
-    )(numbers, *fields, message, one_a, one_b, two_a, two_b, coupling, spread, diag)
+    )(numbers, *fields, message, one_a, one_b, one_c, two_a, two_b, coupling, spread, diag)
 
 
 def solution(mesh):

time: 24.1 us -> 22.8 us (0.946)
  starting transfers between devices: 10.9 us -> 9.06 us
  waiting for transfers between devices: 3.93 us -> 4.63 us
    ppermute x6 -> x7, starting transfers between devices: 10.9 us -> 9.06 us  [move(): return lax.ppermute(block, AXES, pairs)]
    ppermute x6 -> x7, waiting for transfers between devices: 3.93 us -> 4.63 us  [move(): return lax.ppermute(block, AXES, pairs)]
  transfers between devices with their start and end apart: 6 -> 7, of which waited for: 2 -> 3; matrix products, arithmetic and copies ran while one was open for 0% -> 0% of each run, Pallas kernels for 12% -> 12%
where the time goes in v4:
time: 22.8 us; the launch traced here: 22.7 us
  starting transfers between devices  9.06 us (40%)
  Pallas kernels  8.91 us (39%)
  waiting for transfers between devices  4.63 us (20%)
    ppermute x7, starting transfers between devices, move(): return lax.ppermute(block, AXES, pairs)  9.06 us
    ppermute x7, waiting for transfers between devices, move(): return lax.ppermute(block, AXES, pairs)  4.63 us
    pallas_call x1, Pallas kernels, shards(): pl.pallas_call(coarse_kernel, out_shape=f32(capacity, values), in_specs=[...  3.24 us
    pallas_call x1, Pallas kernels, shards(): pl.pallas_call(interior_kernel, out_shape=(bf16(6 * values, 2 * values),...  2.82 us
    pallas_call x1, Pallas kernels, shards(): pl.pallas_call(boundary_kernel, out_shape=(f32(frame, values),) * (3 + DE...  1.86 us
    pallas_call x1, Pallas kernels, shards(): pl.pallas_call(pack_kernel, out_shape=(f32(depth + 8, values), f32(depth...  0.99 us
  transfers between devices with their start and end apart: 7, of which 3 were waited for; matrix products, arithmetic and copies ran while one was open for 0% of the time, Pallas kernels for 12%

profile of v4, /device:TPU:0, one launch (start us, length us, event | category | flops | bytes accessed | tf_op | source)
XLA Modules:
  0.0 22.7 jit_solution(6787795737914866426)
XLA Ops:
  0.0 1.0 %pack.1 = (f32[200,128]{1,0:T(8,128)S(1)}, f32[200,128]{1,0:T(8,128)S(1)}, s32[8,128]{1,0:T(8,128)S(1)}) custom-call(s32[32]{0:T(128)} %count_in.1, f32[512,128]{1,0:T(8,128)} %right_in.3, f32[4,128]{1,0:T(4,128)} %bitcast.1), custom_call_target="tpu_custom_call" | custom-call | tf_op jit(solution)/shard_map/pack/pallas_call | solution.py:424
  1.0 3.1 %collective-permute-start = (f32[200,128]{1,0:T(8,128)S(1)}, f32[200,128]{1,0:T(8,128)S(1)}, u32[]{:S(2)}, u32[]{:S(2)}) collective-permute-start(f32[200,128]{1,0:T(8,128)S(1)} %get-tuple-element.28), channel_id=1, source_target_pairs={{0,1},{1,0},{2,3},{3,2},{4,5},{5,4},{6,7},{7,6},{8,9},{9,8},{10,11... | collective-permute-start | bytes 307208 | tf_op jit(solution)/shard_map/ppermute | solution.py:404
  4.1 3.6 %collective-permute-start.1 = (f32[200,128]{1,0:T(8,128)S(1)}, f32[200,128]{1,0:T(8,128)S(1)}, u32[]{:S(2)}, u32[]{:S(2)}) collective-permute-start(f32[200,128]{1,0:T(8,128)S(1)} %get-tuple-element.29), channel_id=1, source_target_pairs={{1,2},{2,1},{3,4},{4,3},{5,6},{6,5},{7,8},{8,7},{9,10},{10,9},{11,... | collective-permute-start | bytes 307208 | tf_op jit(solution)/shard_map/ppermute | solution.py:404
  7.7 2.8 %interior.1 = (bf16[768,256]{1,0:T(8,128)(2,1)S(1)}, bf16[1024,256]{1,0:T(8,128)(2,1)S(1)}, bf16[256,1024]{1,0:T(8,128)(2,1)S(1)}, f32[8,128]{1,0:T(8,128)S(1)},...) custom-call(s32[8,128]{1,0:T(8,128)S(1)} %get-tuple-element.27.numbe, ...), custom_call_target="tpu_custom_call" | custom-call | tf_op jit(solution)/shard_map/interior/pallas_call | solution.py:445
  10.5 0.0 collective-permute-done.first
  10.5 1.2 %collective-permute-done.1.second = f32[200,128]{1,0:T(8,128)S(1)} collective-permute-done((f32[200,128]{1,0:T(8,128)S(1)}, f32[200,128]{1,0:T(8,128)S(1)}, u32[]{:S(2)}, u32[]{:S(2)}) %collective-permute-start.1) | collective-permute-done | bytes 102432 | tf_op jit(solution)/shard_map/ppermute | solution.py:404
  11.7 1.9 %boundary.1 = (f32[896,128]{1,0:T(8,128)S(1)}, f32[896,128]{1,0:T(8,128)S(1)}, f32[896,128]{1,0:T(8,128)S(1)}, f32[896,128]{1,0:T(8,128)S(1)}, f32[896,128]{1,0:...) custom-call(s32[8,128]{1,0:T(8,128)S(1)} %get-tuple-element.27.numbe, ...), custom_call_target="tpu_custom_call", output_to_operand_aliasing={{0}: (6, {}), {1}: (7, {}), {2}: (8, {}), {3}: (9, {}), {4}... | custom-call | tf_op jit(solution)/shard_map/boundary/pallas_call | solution.py:468
  13.6 0.1 collective-permute-start.4
  13.7 0.1 collective-permute-start.3
  13.7 0.8 %collective-permute-start.2 = (f32[72,128]{1,0:T(8,128)S(1)}, f32[72,128]{1,0:T(8,128)S(1)}, u32[]{:S(2)}, u32[]{:S(2)}) collective-permute-start(f32[72,128]{1,0:T(8,128)S(1)} %get-tuple-element.45.rest_3_), channel_id=1, source_target_pairs={{0,1},{1,0},{2,3},{3,2},{4,5},{5,4},{6,7},{7,6},{8,9},{9,8},{10,11... | collective-permute-start | bytes 110600 | tf_op jit(solution)/shard_map/ppermute | solution.py:404
  14.6 1.0 %collective-permute-start.5 = (f32[56,128]{1,0:T(8,128)S(1)}, f32[56,128]{1,0:T(8,128)S(1)}, u32[]{:S(2)}, u32[]{:S(2)}) collective-permute-start(f32[56,128]{1,0:T(8,128)S(1)} %get-tuple-element.46), channel_id=1, source_target_pairs={{0,2},{2,0},{1,3},{3,1},{4,6},{6,4},{5,7},{7,5},{8,10},{10,8},{9,1... | collective-permute-start | bytes 86024 | tf_op jit(solution)/shard_map/ppermute | solution.py:404
  15.5 0.5 %collective-permute-start.6 = (f32[56,128]{1,0:T(8,128)S(1)}, f32[56,128]{1,0:T(8,128)S(1)}, u32[]{:S(2)}, u32[]{:S(2)}) collective-permute-start(f32[56,128]{1,0:T(8,128)S(1)} %get-tuple-element.47), channel_id=1, source_target_pairs={{2,4},{4,2},{3,5},{5,3},{6,8},{8,6},{7,9},{9,7},{10,12},{12,10},{1... | collective-permute-start | bytes 86024 | tf_op jit(solution)/shard_map/ppermute | solution.py:404
  16.0 0.4 %collective-permute-done.5.rest_7_ = f32[56,128]{1,0:T(8,128)S(1)} collective-permute-done((f32[56,128]{1,0:T(8,128)S(1)}, f32[56,128]{1,0:T(8,128)S(1)}, u32[]{:S(2)}, u32[]{:S(2)}) %collective-permute-start.5) | collective-permute-done | bytes 28704 | tf_op jit(solution)/shard_map/ppermute | solution.py:404
  16.4 3.0 %collective-permute-done.6.rest_8_ = f32[56,128]{1,0:T(8,128)S(1)} collective-permute-done((f32[56,128]{1,0:T(8,128)S(1)}, f32[56,128]{1,0:T(8,128)S(1)}, u32[]{:S(2)}, u32[]{:S(2)}) %collective-permute-start.6) | collective-permute-done | bytes 28704 | tf_op jit(solution)/shard_map/ppermute | solution.py:404
  19.4 0.0 collective-permute-done.4.rest_6_
  19.4 0.0 collective-permute-done.3.rest_5_
  19.4 0.0 collective-permute-done.2.rest_4_
  19.4 3.2 %coarse.1 = f32[512,128]{1,0:T(8,128)} custom-call(s32[8,128]{1,0:T(8,128)S(1)} %get-tuple-element.27.numbers, f32[896,128]{1,0:T(8,128)S(1)} %get-tuple-element.39.residual, f32[896,128]{1,0:T(8,128)S(1)} %get-tuple-element.40.coef, f32[896,128]{1,0:T(8,128)S(1)} %get-tuple-element.41.jacobi, f32[896,128]{1,0:T(8,128)S(1)} %get-tuple-element.42.rest_0_, ...), custom_call_target="tpu_custom_call" | custom-call | tf_op jit(solution)/shard_map/coarse/pallas_call | solution.py:493
Async XLA Ops:
  1.0 9.5 %collective-permute-start = (f32[200,128]{1,0:T(8,128)S(1)}, f32[200,128]{1,0:T(8,128)S(1)}, u32[]{:S(2)}, u32[]{:S(2)}) collective-permute-start(f32[200,128]{1,0:T(8,128)S(1)} %get-tuple-element.28), channel_id=1, source_target_pairs={{0,1},{1,0},{2,3},{3,2},{4,5},{5,4},{6,7},{7,6},{8,9},{9,8},{10,11... | collective-permute-start | bytes 307208 | tf_op jit(solution)/shard_map/ppermute | solution.py:404
  4.1 7.7 %collective-permute-start.1 = (f32[200,128]{1,0:T(8,128)S(1)}, f32[200,128]{1,0:T(8,128)S(1)}, u32[]{:S(2)}, u32[]{:S(2)}) collective-permute-start(f32[200,128]{1,0:T(8,128)S(1)} %get-tuple-element.29), channel_id=1, source_target_pairs={{1,2},{2,1},{3,4},{4,3},{5,6},{6,5},{7,8},{8,7},{9,10},{10,9},{11,... | collective-permute-start | bytes 307208 | tf_op jit(solution)/shard_map/ppermute | solution.py:404
  13.6 5.8 %collective-permute-start.4 = (f32[72,128]{1,0:T(8,128)S(1)}, f32[72,128]{1,0:T(8,128)S(1)}, u32[]{:S(2)}, u32[]{:S(2)}) collective-permute-start(f32[72,128]{1,0:T(8,128)S(1)} %get-tuple-element.45.rest_3_), channel_id=1, source_target_pairs={{1,2},{2,1},{0,3},{3,0},{30,29},{29,30},{31,28},{28,31},{4,6},{5,7... | collective-permute-start | bytes 110600 | tf_op jit(solution)/shard_map/ppermute | solution.py:404
  13.7 5.7 %collective-permute-start.3 = (f32[72,128]{1,0:T(8,128)S(1)}, f32[72,128]{1,0:T(8,128)S(1)}, u32[]{:S(2)}, u32[]{:S(2)}) collective-permute-start(f32[72,128]{1,0:T(8,128)S(1)} %get-tuple-element.45.rest_3_), channel_id=1, source_target_pairs={{0,1},{1,2},{2,0},{29,30},{30,31},{31,29},{3,4},{4,3},{5,6},{6,5},... | collective-permute-start | bytes 110600 | tf_op jit(solution)/shard_map/ppermute | solution.py:404
  13.7 5.7 %collective-permute-start.2 = (f32[72,128]{1,0:T(8,128)S(1)}, f32[72,128]{1,0:T(8,128)S(1)}, u32[]{:S(2)}, u32[]{:S(2)}) collective-permute-start(f32[72,128]{1,0:T(8,128)S(1)} %get-tuple-element.45.rest_3_), channel_id=1, source_target_pairs={{0,1},{1,0},{2,3},{3,2},{4,5},{5,4},{6,7},{7,6},{8,9},{9,8},{10,11... | collective-permute-start | bytes 110600 | tf_op jit(solution)/shard_map/ppermute | solution.py:404
  14.6 1.8 %collective-permute-start.5 = (f32[56,128]{1,0:T(8,128)S(1)}, f32[56,128]{1,0:T(8,128)S(1)}, u32[]{:S(2)}, u32[]{:S(2)}) collective-permute-start(f32[56,128]{1,0:T(8,128)S(1)} %get-tuple-element.46), channel_id=1, source_target_pairs={{0,2},{2,0},{1,3},{3,1},{4,6},{6,4},{5,7},{7,5},{8,10},{10,8},{9,1... | collective-permute-start | bytes 86024 | tf_op jit(solution)/shard_map/ppermute | solution.py:404
  15.5 3.9 %collective-permute-start.6 = (f32[56,128]{1,0:T(8,128)S(1)}, f32[56,128]{1,0:T(8,128)S(1)}, u32[]{:S(2)}, u32[]{:S(2)}) collective-permute-start(f32[56,128]{1,0:T(8,128)S(1)} %get-tuple-element.47), channel_id=1, source_target_pairs={{2,4},{4,2},{3,5},{5,3},{6,8},{8,6},{7,9},{9,7},{10,12},{12,10},{1... | collective-permute-start | bytes 86024 | tf_op jit(solution)/shard_map/ppermute | solution.py:404

commit v5 on v4

--- a/solution.py
+++ b/solution.py
@@ -37,7 +37,7 @@
 
 
 def is_near_end(device, total):
-    return (device == 1) | (device == 2) | (device == total - 3) | (device == total - 2)
+    return (device == 2) | (device == total - 3)
 
 
 def halves(value):
@@ -208,7 +208,7 @@
 
 
 def boundary_kernel(
-    numbers, first, second, coupling, restrict, diag, *fields
+    numbers, first, second, third, coupling, restrict, diag, *fields
 ):
     residual, coef, jacobi = fields[DEG + 3 : DEG + 6]
     updates = fields[DEG + 6 : 2 * DEG + 6]
@@ -222,8 +222,9 @@
     is_even = device % 2 == 0
     end = pl.multiple_of(depth + scalar_of(numbers, NEAR_CELLS), 8)
     diagonal = diag[0:1, :]
-    left = jnp.where(is_even, second[...], first[...])
-    right = jnp.where(is_even, first[...], second[...])
+    odd = jnp.where(is_near_end(device, total), third[...], second[...])
+    left = jnp.where(is_even, odd, first[...])
+    right = jnp.where(is_even, first[...], odd)
     keep, gain = STEPS[0]
     for side, start, exists in ((left, 0, device > 0), (right, end, device < total - 1)):
         pieces = []
@@ -440,7 +441,17 @@
         name="pack",
         compiler_params=params,
     )(off_chip(fine_count), off_chip(right_side), off_chip(coef_rows))
-    second_in = exchange(second, 1, 1, True)
+    total = lax.axis_size(AXES)
+    ring = [(0, 2), (2, 1), (1, 0)]
+    ring += [(total - 1 - source, total - 1 - target) for source, target in ring]
+    for device in range(3, total - 3, 2):
+        ring += [(device, device + 1), (device + 1, device)]
+    ends = [(1, 2), (2, 0), (0, 3), (3, 1)]
+    ends += [(total - 1 - source, total - 1 - target) for source, target in ends]
+    for device in range(4, total - 4):
+        ends += [(device, device + 2 if device % 4 < 2 else device - 2)]
+    second_in = move(second, ring)
+    third_in = move(second, ends)
     first_in = exchange(first, 1, 0, False)
     prepared = pl.pallas_call(
         interior_kernel,
@@ -469,22 +480,14 @@
         boundary_kernel,
         out_shape=(f32(frame, values),) * (3 + DEG)
         + (f32(slots + 8, values), f32(far, values), f32(far, values)),
-        in_specs=[vmem] * (9 + DEG),
+        in_specs=[vmem] * (10 + DEG),
         out_specs=(vmem,) * (6 + DEG),
         scratch_shapes=[buffer(slots + 2 * margin, values), buffer(values, values)],
-        input_output_aliases={6 + index: index for index in range(3 + DEG)},
+        input_output_aliases={7 + index: index for index in range(3 + DEG)},
         name="boundary",
         compiler_params=params,
-    )(numbers, first_in, second_in, coupling, restrict, diag, *prepared[4:])
-    total = lax.axis_size(AXES)
-    ring = [(0, 1), (1, 2), (2, 0), (total - 3, total - 2), (total - 2, total - 1), (total - 1, total - 3)]
-    for device in range(3, total - 3, 2):
-        ring += [(device, device + 1), (device + 1, device)]
+    )(numbers, first_in, second_in, third_in, coupling, restrict, diag, *prepared[4:])
     one_b = move(message, ring)
-    ends = [(1, 2), (2, 1), (0, 3), (3, 0)]
-    ends += [(total - 1 - source, total - 1 - target) for source, target in ends]
-    for device in range(4, total - 4):
-        ends += [(device, device + 2 if device % 4 < 2 else device - 2)]
     one_c = move(message, ends)
     two_b = exchange(far_odd, 2, 1, True)
     one_a = exchange(message, 1, 0, False)

time: 22.8 us -> 22.7 us (level)
  starting transfers between devices: 9.06 us -> 7.57 us
  waiting for transfers between devices: 4.63 us -> 5.99 us
    ppermute x7 -> x8, starting transfers between devices: 9.06 us -> 7.57 us  [move(): return lax.ppermute(block, AXES, pairs)]
    ppermute x7 -> x8, waiting for transfers between devices: 4.63 us -> 5.99 us  [move(): return lax.ppermute(block, AXES, pairs)]
  transfers between devices with their start and end apart: 7 -> 8, of which waited for: 3 -> 4; matrix products, arithmetic and copies ran while one was open for 0% -> 0% of each run, Pallas kernels for 12% -> 13%
where the time goes in v5:
time: 22.7 us; the launch traced here: 22.5 us
  Pallas kernels  8.9 us (39%)
  starting transfers between devices  7.57 us (33%)
  waiting for transfers between devices  5.99 us (26%)
    ppermute x8, starting transfers between devices, move(): return lax.ppermute(block, AXES, pairs)  7.57 us
    ppermute x8, waiting for transfers between devices, move(): return lax.ppermute(block, AXES, pairs)  5.99 us
    pallas_call x1, Pallas kernels, shards(): pl.pallas_call(coarse_kernel, out_shape=f32(capacity, values), in_specs=[...  3.23 us
    pallas_call x1, Pallas kernels, shards(): pl.pallas_call(interior_kernel, out_shape=(bf16(6 * values, 2 * values),...  2.82 us
    pallas_call x1, Pallas kernels, shards(): pl.pallas_call(boundary_kernel, out_shape=(f32(frame, values),) * (3 + DE...  1.86 us
    pallas_call x1, Pallas kernels, shards(): pl.pallas_call(pack_kernel, out_shape=(f32(depth + 8, values), f32(depth...  0.99 us
  transfers between devices with their start and end apart: 8, of which 4 were waited for; matrix products, arithmetic and copies ran while one was open for 0% of the time, Pallas kernels for 13%

profile of v5, /device:TPU:0, one launch (start us, length us, event | category | flops | bytes accessed | tf_op | source)
XLA Modules:
  0.0 22.5 jit_solution(8751525723434694676)
XLA Ops:
  0.0 1.0 %pack.1 = (f32[200,128]{1,0:T(8,128)S(1)}, f32[200,128]{1,0:T(8,128)S(1)}, s32[8,128]{1,0:T(8,128)S(1)}) custom-call(s32[32]{0:T(128)} %count_in.1, f32[512,128]{1,0:T(8,128)} %right_in.3, f32[4,128]{1,0:T(4,128)} %bitcast.1), custom_call_target="tpu_custom_call" | custom-call | tf_op jit(solution)/shard_map/pack/pallas_call | solution.py:425
  1.0 3.1 %collective-permute-start = (f32[200,128]{1,0:T(8,128)S(1)}, f32[200,128]{1,0:T(8,128)S(1)}, u32[]{:S(2)}, u32[]{:S(2)}) collective-permute-start(f32[200,128]{1,0:T(8,128)S(1)} %get-tuple-element.28), channel_id=1, source_target_pairs={{0,1},{1,0},{2,3},{3,2},{4,5},{5,4},{6,7},{7,6},{8,9},{9,8},{10,11... | collective-permute-start | bytes 307208 | tf_op jit(solution)/shard_map/ppermute | solution.py:405
  4.1 0.0 collective-permute-start.2
  4.1 0.5 %collective-permute-start.1 = (f32[200,128]{1,0:T(8,128)S(1)}, f32[200,128]{1,0:T(8,128)S(1)}, u32[]{:S(2)}, u32[]{:S(2)}) collective-permute-start(f32[200,128]{1,0:T(8,128)S(1)} %get-tuple-element.29), channel_id=1, source_target_pairs={{0,2},{2,1},{1,0},{31,29},{29,30},{30,31},{3,4},{4,3},{5,6},{6,5},... | collective-permute-start | bytes 307208 | tf_op jit(solution)/shard_map/ppermute | solution.py:405
  4.6 2.8 %interior.1 = (bf16[768,256]{1,0:T(8,128)(2,1)S(1)}, bf16[1024,256]{1,0:T(8,128)(2,1)S(1)}, bf16[256,1024]{1,0:T(8,128)(2,1)S(1)}, f32[8,128]{1,0:T(8,128)S(1)},...) custom-call(s32[8,128]{1,0:T(8,128)S(1)} %get-tuple-element.27.numbe, ...), custom_call_target="tpu_custom_call" | custom-call | tf_op jit(solution)/shard_map/interior/pallas_call | solution.py:456
  7.4 0.3 %collective-permute-done.first = f32[200,128]{1,0:T(8,128)S(1)} collective-permute-done((f32[200,128]{1,0:T(8,128)S(1)}, f32[200,128]{1,0:T(8,128)S(1)}, u32[]{:S(2)}, u32[]{:S(2)}) %collective-permute-start) | collective-permute-done | bytes 102432 | tf_op jit(solution)/shard_map/ppermute | solution.py:405
  7.7 1.9 %collective-permute-done.2.third = f32[200,128]{1,0:T(8,128)S(1)} collective-permute-done((f32[200,128]{1,0:T(8,128)S(1)}, f32[200,128]{1,0:T(8,128)S(1)}, u32[]{:S(2)}, u32[]{:S(2)}) %collective-permute-start.2) | collective-permute-done | bytes 102432 | tf_op jit(solution)/shard_map/ppermute | solution.py:405
  9.5 0.0 collective-permute-done.1.second
  9.5 1.9 %boundary.1 = (f32[896,128]{1,0:T(8,128)S(1)}, f32[896,128]{1,0:T(8,128)S(1)}, f32[896,128]{1,0:T(8,128)S(1)}, f32[896,128]{1,0:T(8,128)S(1)}, f32[896,128]{1,0:...) custom-call(s32[8,128]{1,0:T(8,128)S(1)} %get-tuple-element.27.numbe, ...), custom_call_target="tpu_custom_call", output_to_operand_aliasing={{0}: (7, {}), {1}: (8, {}), {2}: (9, {}), {3}: (10, {}), {4... | custom-call | tf_op jit(solution)/shard_map/boundary/pallas_call | solution.py:479
  11.4 1.9 %collective-permute-start.5 = (f32[72,128]{1,0:T(8,128)S(1)}, f32[72,128]{1,0:T(8,128)S(1)}, u32[]{:S(2)}, u32[]{:S(2)}) collective-permute-start(f32[72,128]{1,0:T(8,128)S(1)} %get-tuple-element.45.rest_3_), channel_id=1, source_target_pairs={{1,2},{2,0},{0,3},{3,1},{30,29},{29,31},{31,28},{28,30},{4,6},{5,7... | collective-permute-start | bytes 110600 | tf_op jit(solution)/shard_map/ppermute | solution.py:405
  13.3 0.0 collective-permute-start.4
  13.3 2.0 %collective-permute-start.3 = (f32[72,128]{1,0:T(8,128)S(1)}, f32[72,128]{1,0:T(8,128)S(1)}, u32[]{:S(2)}, u32[]{:S(2)}) collective-permute-start(f32[72,128]{1,0:T(8,128)S(1)} %get-tuple-element.45.rest_3_), channel_id=1, source_target_pairs={{0,1},{1,0},{2,3},{3,2},{4,5},{5,4},{6,7},{7,6},{8,9},{9,8},{10,11... | collective-permute-start | bytes 110600 | tf_op jit(solution)/shard_map/ppermute | solution.py:405
  15.4 0.0 collective-permute-start.6
  15.4 0.0 collective-permute-start.7
  15.4 1.2 %collective-permute-done.6.rest_7_ = f32[56,128]{1,0:T(8,128)S(1)} collective-permute-done((f32[56,128]{1,0:T(8,128)S(1)}, f32[56,128]{1,0:T(8,128)S(1)}, u32[]{:S(2)}, u32[]{:S(2)}) %collective-permute-start.6) | collective-permute-done | bytes 28704 | tf_op jit(solution)/shard_map/ppermute | solution.py:405
  16.6 2.7 %collective-permute-done.7.rest_8_ = f32[56,128]{1,0:T(8,128)S(1)} collective-permute-done((f32[56,128]{1,0:T(8,128)S(1)}, f32[56,128]{1,0:T(8,128)S(1)}, u32[]{:S(2)}, u32[]{:S(2)}) %collective-permute-start.7) | collective-permute-done | bytes 28704 | tf_op jit(solution)/shard_map/ppermute | solution.py:405
  19.2 0.0 collective-permute-done.5.rest_6_
  19.3 0.0 collective-permute-done.4.rest_5_
  19.3 0.0 collective-permute-done.3.rest_4_
  19.3 3.2 %coarse.1 = f32[512,128]{1,0:T(8,128)} custom-call(s32[8,128]{1,0:T(8,128)S(1)} %get-tuple-element.27.numbers, f32[896,128]{1,0:T(8,128)S(1)} %get-tuple-element.39.residual, f32[896,128]{1,0:T(8,128)S(1)} %get-tuple-element.40.coef, f32[896,128]{1,0:T(8,128)S(1)} %get-tuple-element.41.jacobi, f32[896,128]{1,0:T(8,128)S(1)} %get-tuple-element.42.rest_0_, ...), custom_call_target="tpu_custom_call" | custom-call | tf_op jit(solution)/shard_map/coarse/pallas_call | solution.py:496
Async XLA Ops:
  1.0 6.7 %collective-permute-start = (f32[200,128]{1,0:T(8,128)S(1)}, f32[200,128]{1,0:T(8,128)S(1)}, u32[]{:S(2)}, u32[]{:S(2)}) collective-permute-start(f32[200,128]{1,0:T(8,128)S(1)} %get-tuple-element.28), channel_id=1, source_target_pairs={{0,1},{1,0},{2,3},{3,2},{4,5},{5,4},{6,7},{7,6},{8,9},{9,8},{10,11... | collective-permute-start | bytes 307208 | tf_op jit(solution)/shard_map/ppermute | solution.py:405
  4.1 5.5 %collective-permute-start.2 = (f32[200,128]{1,0:T(8,128)S(1)}, f32[200,128]{1,0:T(8,128)S(1)}, u32[]{:S(2)}, u32[]{:S(2)}) collective-permute-start(f32[200,128]{1,0:T(8,128)S(1)} %get-tuple-element.29), channel_id=1, source_target_pairs={{1,2},{2,0},{0,3},{3,1},{30,29},{29,31},{31,28},{28,30},{4,6},{5,7... | collective-permute-start | bytes 307208 | tf_op jit(solution)/shard_map/ppermute | solution.py:405
  4.1 5.5 %collective-permute-start.1 = (f32[200,128]{1,0:T(8,128)S(1)}, f32[200,128]{1,0:T(8,128)S(1)}, u32[]{:S(2)}, u32[]{:S(2)}) collective-permute-start(f32[200,128]{1,0:T(8,128)S(1)} %get-tuple-element.29), channel_id=1, source_target_pairs={{0,2},{2,1},{1,0},{31,29},{29,30},{30,31},{3,4},{4,3},{5,6},{6,5},... | collective-permute-start | bytes 307208 | tf_op jit(solution)/shard_map/ppermute | solution.py:405
  11.4 7.9 %collective-permute-start.5 = (f32[72,128]{1,0:T(8,128)S(1)}, f32[72,128]{1,0:T(8,128)S(1)}, u32[]{:S(2)}, u32[]{:S(2)}) collective-permute-start(f32[72,128]{1,0:T(8,128)S(1)} %get-tuple-element.45.rest_3_), channel_id=1, source_target_pairs={{1,2},{2,0},{0,3},{3,1},{30,29},{29,31},{31,28},{28,30},{4,6},{5,7... | collective-permute-start | bytes 110600 | tf_op jit(solution)/shard_map/ppermute | solution.py:405
  13.3 5.9 %collective-permute-start.4 = (f32[72,128]{1,0:T(8,128)S(1)}, f32[72,128]{1,0:T(8,128)S(1)}, u32[]{:S(2)}, u32[]{:S(2)}) collective-permute-start(f32[72,128]{1,0:T(8,128)S(1)} %get-tuple-element.45.rest_3_), channel_id=1, source_target_pairs={{0,2},{2,1},{1,0},{31,29},{29,30},{30,31},{3,4},{4,3},{5,6},{6,5},... | collective-permute-start | bytes 110600 | tf_op jit(solution)/shard_map/ppermute | solution.py:405
  13.3 5.9 %collective-permute-start.3 = (f32[72,128]{1,0:T(8,128)S(1)}, f32[72,128]{1,0:T(8,128)S(1)}, u32[]{:S(2)}, u32[]{:S(2)}) collective-permute-start(f32[72,128]{1,0:T(8,128)S(1)} %get-tuple-element.45.rest_3_), channel_id=1, source_target_pairs={{0,1},{1,0},{2,3},{3,2},{4,5},{5,4},{6,7},{7,6},{8,9},{9,8},{10,11... | collective-permute-start | bytes 110600 | tf_op jit(solution)/shard_map/ppermute | solution.py:405
  15.4 1.2 %collective-permute-start.6 = (f32[56,128]{1,0:T(8,128)S(1)}, f32[56,128]{1,0:T(8,128)S(1)}, u32[]{:S(2)}, u32[]{:S(2)}) collective-permute-start(f32[56,128]{1,0:T(8,128)S(1)} %get-tuple-element.46), channel_id=1, source_target_pairs={{0,2},{2,0},{1,3},{3,1},{4,6},{6,4},{5,7},{7,5},{8,10},{10,8},{9,1... | collective-permute-start | bytes 86024 | tf_op jit(solution)/shard_map/ppermute | solution.py:405
  15.4 3.9 %collective-permute-start.7 = (f32[56,128]{1,0:T(8,128)S(1)}, f32[56,128]{1,0:T(8,128)S(1)}, u32[]{:S(2)}, u32[]{:S(2)}) collective-permute-start(f32[56,128]{1,0:T(8,128)S(1)} %get-tuple-element.47), channel_id=1, source_target_pairs={{2,4},{4,2},{3,5},{5,3},{6,8},{8,6},{7,9},{9,7},{10,12},{12,10},{1... | collective-permute-start | bytes 86024 | tf_op jit(solution)/shard_map/ppermute | solution.py:405

commit v6 on v5

--- a/solution.py
+++ b/solution.py
@@ -127,7 +127,7 @@
 
 def interior_kernel(
     numbers, right_in, coef_in, cell_in, near_in, far_in, prolong_in,
-    coupling, restrict, spread, diag, residual, coef, jacobi, *rest,
+    coupling, restrict, diag, residual, coef, jacobi, *rest,
 ):
     updates = rest[:DEG]
     coef_rows, cell_matrix, face_near, face_far, prolong, arrivals = rest[DEG:]
@@ -199,12 +199,18 @@
     for child in range(CHILDREN):
         rows = pl.ds(child * values, values)
         block = prolong[child]
-        high, low = halves(block)
-        spread[:values, rows] = high
-        spread[values:, rows] = low
         high, low = halves(jnp.transpose(block))
         restrict[rows, :values] = high
         restrict[rows, values:] = low
+
+
+def spread_kernel(prolong, spread):
+    values = prolong.shape[1]
+    for child in range(CHILDREN):
+        columns_of = pl.ds(child * values, values)
+        high, low = halves(prolong[child])
+        spread[:values, columns_of] = high
+        spread[values:, columns_of] = low
 
 
 def boundary_kernel(
@@ -458,12 +464,11 @@
         out_shape=(
             bf16(6 * values, 2 * values),
             bf16(CHILDREN * values, 2 * values),
-            bf16(2 * values, CHILDREN * values),
             f32(8, values),
         )
         + (f32(frame, values),) * (3 + DEG),
         in_specs=[vmem] + [hbm] * 6,
-        out_specs=(vmem,) * (7 + DEG),
+        out_specs=(vmem,) * (6 + DEG),
         scratch_shapes=[
             buffer(*coef_rows.shape),
             buffer(values, values),
@@ -475,7 +480,7 @@
         name="interior",
         compiler_params=params,
     )(numbers, *(off_chip(each) for each in (right_side, coef_rows, cell_matrix, face_near, face_far, prolong)))
-    coupling, restrict, spread, diag = prepared[:4]
+    coupling, restrict, diag = prepared[:3]
     *fields, message, far_even, far_odd = pl.pallas_call(
         boundary_kernel,
         out_shape=(f32(frame, values),) * (3 + DEG)
@@ -486,12 +491,20 @@
         input_output_aliases={7 + index: index for index in range(3 + DEG)},
         name="boundary",
         compiler_params=params,
-    )(numbers, first_in, second_in, third_in, coupling, restrict, diag, *prepared[4:])
+    )(numbers, first_in, second_in, third_in, coupling, restrict, diag, *prepared[3:])
     one_b = move(message, ring)
     one_c = move(message, ends)
     two_b = exchange(far_odd, 2, 1, True)
     one_a = exchange(message, 1, 0, False)
     two_a = exchange(far_even, 2, 0, False)
+    spread = pl.pallas_call(
+        spread_kernel,
+        out_shape=bf16(2 * values, CHILDREN * values),
+        in_specs=[vmem],
+        out_specs=vmem,
+        name="spread",
+        compiler_params=params,
+    )(prolong)
     coarse_frame = 4 * slots + 4 * margin
     return pl.pallas_call(
         coarse_kernel,

time: 22.7 us -> 23.4 us (1.031)
  starting transfers between devices: 7.57 us -> 9.86 us
  waiting for transfers between devices: 5.99 us -> 4.32 us
    ppermute x8, starting transfers between devices: 7.57 us -> 9.86 us  [move(): return lax.ppermute(block, AXES, pairs)]
    ppermute x8, waiting for transfers between devices: 5.99 us -> 4.32 us  [move(): return lax.ppermute(block, AXES, pairs)]
where the time goes in v6:
time: 23.4 us; the launch traced here: 23.2 us
  starting transfers between devices  9.86 us (42%)
  Pallas kernels  9.01 us (39%)
  waiting for transfers between devices  4.32 us (18%)
    ppermute x8, starting transfers between devices, move(): return lax.ppermute(block, AXES, pairs)  9.86 us
    ppermute x8, waiting for transfers between devices, move(): return lax.ppermute(block, AXES, pairs)  4.32 us
    pallas_call x1, Pallas kernels, shards(): pl.pallas_call(coarse_kernel, out_shape=f32(capacity, values), in_specs=[...  3.2 us
    pallas_call x1, Pallas kernels, shards(): pl.pallas_call(interior_kernel, out_shape=(bf16(6 * values, 2 * values),...  2.82 us
    pallas_call x1, Pallas kernels, shards(): pl.pallas_call(boundary_kernel, out_shape=(f32(frame, values),) * (3 + DE...  1.87 us
    pallas_call x1, Pallas kernels, shards(): pl.pallas_call(pack_kernel, out_shape=(f32(depth + 8, values), f32(depth...  0.99 us
  transfers between devices with their start and end apart: 8, of which 4 were waited for; matrix products, arithmetic and copies ran while one was open for 0% of the time, Pallas kernels for 13%

profile of v6, /device:TPU:0, one launch (start us, length us, event | category | flops | bytes accessed | tf_op | source)
XLA Modules:
  0.0 23.2 jit_solution(1817131792355654873)
XLA Ops:
  0.0 1.0 %pack.1 = (f32[200,128]{1,0:T(8,128)S(1)}, f32[200,128]{1,0:T(8,128)S(1)}, s32[8,128]{1,0:T(8,128)S(1)}) custom-call(s32[32]{0:T(128)} %count_in.1, f32[512,128]{1,0:T(8,128)} %right_in.3, f32[4,128]{1,0:T(4,128)} %bitcast.1), custom_call_target="tpu_custom_call" | custom-call | tf_op jit(solution)/shard_map/pack/pallas_call | solution.py:431
  1.0 0.5 %collective-permute-start.1 = (f32[200,128]{1,0:T(8,128)S(1)}, f32[200,128]{1,0:T(8,128)S(1)}, u32[]{:S(2)}, u32[]{:S(2)}) collective-permute-start(f32[200,128]{1,0:T(8,128)S(1)} %get-tuple-element.28), channel_id=1, source_target_pairs={{0,2},{2,1},{1,0},{31,29},{29,30},{30,31},{3,4},{4,3},{5,6},{6,5},... | collective-permute-start | bytes 307208 | tf_op jit(solution)/shard_map/ppermute | solution.py:411
  1.5 3.7 %collective-permute-start.2 = (f32[200,128]{1,0:T(8,128)S(1)}, f32[200,128]{1,0:T(8,128)S(1)}, u32[]{:S(2)}, u32[]{:S(2)}) collective-permute-start(f32[200,128]{1,0:T(8,128)S(1)} %get-tuple-element.28), channel_id=1, source_target_pairs={{1,2},{2,0},{0,3},{3,1},{30,29},{29,31},{31,28},{28,30},{4,6},{5,7... | collective-permute-start | bytes 307208 | tf_op jit(solution)/shard_map/ppermute | solution.py:411
  5.2 0.6 %collective-permute-start = (f32[200,128]{1,0:T(8,128)S(1)}, f32[200,128]{1,0:T(8,128)S(1)}, u32[]{:S(2)}, u32[]{:S(2)}) collective-permute-start(f32[200,128]{1,0:T(8,128)S(1)} %get-tuple-element.27), channel_id=1, source_target_pairs={{0,1},{1,0},{2,3},{3,2},{4,5},{5,4},{6,7},{7,6},{8,9},{9,8},{10,11... | collective-permute-start | bytes 307208 | tf_op jit(solution)/shard_map/ppermute | solution.py:411
  5.8 2.8 %interior.1 = (bf16[768,256]{1,0:T(8,128)(2,1)S(1)}, bf16[1024,256]{1,0:T(8,128)(2,1)S(1)}, f32[8,128]{1,0:T(8,128)S(1)}, f32[896,128]{1,0:T(8,128)S(1)}, f32[89...) custom-call(s32[8,128]{1,0:T(8,128)S(1)} %get-tuple-element.26.numbe, ...), custom_call_target="tpu_custom_call" | custom-call | tf_op jit(solution)/shard_map/interior/pallas_call | solution.py:462
  8.6 0.0 collective-permute-done.1.second
  8.6 0.2 collective-permute-done.2.third
  8.9 1.2 %collective-permute-done.first = f32[200,128]{1,0:T(8,128)S(1)} collective-permute-done((f32[200,128]{1,0:T(8,128)S(1)}, f32[200,128]{1,0:T(8,128)S(1)}, u32[]{:S(2)}, u32[]{:S(2)}) %collective-permute-start) | collective-permute-done | bytes 102432 | tf_op jit(solution)/shard_map/ppermute | solution.py:411
  10.0 0.0 copy-start
  10.1 1.9 %boundary.1 = (f32[896,128]{1,0:T(8,128)S(1)}, f32[896,128]{1,0:T(8,128)S(1)}, f32[896,128]{1,0:T(8,128)S(1)}, f32[896,128]{1,0:T(8,128)S(1)}, f32[896,128]{1,0:...) custom-call(s32[8,128]{1,0:T(8,128)S(1)} %get-tuple-element.26.numbe, ...), custom_call_target="tpu_custom_call", output_to_operand_aliasing={{0}: (7, {}), {1}: (8, {}), {2}: (9, {}), {3}: (10, {}), {4... | custom-call | tf_op jit(solution)/shard_map/boundary/pallas_call | solution.py:484
  11.9 2.5 %collective-permute-start.3 = (f32[72,128]{1,0:T(8,128)S(1)}, f32[72,128]{1,0:T(8,128)S(1)}, u32[]{:S(2)}, u32[]{:S(2)}) collective-permute-start(f32[72,128]{1,0:T(8,128)S(1)} %get-tuple-element.44.rest_3_), channel_id=1, source_target_pairs={{0,1},{1,0},{2,3},{3,2},{4,5},{5,4},{6,7},{7,6},{8,9},{9,8},{10,11... | collective-permute-start | bytes 110600 | tf_op jit(solution)/shard_map/ppermute | solution.py:411
  14.5 0.0 collective-permute-start.4
  14.5 1.7 %collective-permute-start.5 = (f32[72,128]{1,0:T(8,128)S(1)}, f32[72,128]{1,0:T(8,128)S(1)}, u32[]{:S(2)}, u32[]{:S(2)}) collective-permute-start(f32[72,128]{1,0:T(8,128)S(1)} %get-tuple-element.44.rest_3_), channel_id=1, source_target_pairs={{1,2},{2,0},{0,3},{3,1},{30,29},{29,31},{31,28},{28,30},{4,6},{5,7... | collective-permute-start | bytes 110600 | tf_op jit(solution)/shard_map/ppermute | solution.py:411
  16.2 0.0 collective-permute-start.6
  16.2 0.8 %collective-permute-start.7 = (f32[56,128]{1,0:T(8,128)S(1)}, f32[56,128]{1,0:T(8,128)S(1)}, u32[]{:S(2)}, u32[]{:S(2)}) collective-permute-start(f32[56,128]{1,0:T(8,128)S(1)} %get-tuple-element.46), channel_id=1, source_target_pairs={{2,4},{4,2},{3,5},{5,3},{6,8},{8,6},{7,9},{9,7},{10,12},{12,10},{1... | collective-permute-start | bytes 86024 | tf_op jit(solution)/shard_map/ppermute | solution.py:411
  17.0 0.0 copy-done
  17.0 0.1 spread.1.rest_10_
  17.1 0.2 collective-permute-done.6.rest_7_
  17.4 2.7 %collective-permute-done.7.rest_8_ = f32[56,128]{1,0:T(8,128)S(1)} collective-permute-done((f32[56,128]{1,0:T(8,128)S(1)}, f32[56,128]{1,0:T(8,128)S(1)}, u32[]{:S(2)}, u32[]{:S(2)}) %collective-permute-start.7) | collective-permute-done | bytes 28704 | tf_op jit(solution)/shard_map/ppermute | solution.py:411
  20.0 0.0 collective-permute-done.3.rest_4_
  20.0 0.0 collective-permute-done.4.rest_5_
  20.0 0.0 collective-permute-done.5.rest_6_
  20.0 3.2 %coarse.1 = f32[512,128]{1,0:T(8,128)} custom-call(s32[8,128]{1,0:T(8,128)S(1)} %get-tuple-element.26.numbers, f32[896,128]{1,0:T(8,128)S(1)} %get-tuple-element.38.residual, f32[896,128]{1,0:T(8,128)S(1)} %get-tuple-element.39.coef, f32[896,128]{1,0:T(8,128)S(1)} %get-tuple-element.40.jacobi, f32[896,128]{1,0:T(8,128)S(1)} %get-tuple-element.41.rest_0_, ...), custom_call_target="tpu_custom_call" | custom-call | tf_op jit(solution)/shard_map/coarse/pallas_call | solution.py:509
Async XLA Ops:
  1.0 7.6 %collective-permute-start.1 = (f32[200,128]{1,0:T(8,128)S(1)}, f32[200,128]{1,0:T(8,128)S(1)}, u32[]{:S(2)}, u32[]{:S(2)}) collective-permute-start(f32[200,128]{1,0:T(8,128)S(1)} %get-tuple-element.28), channel_id=1, source_target_pairs={{0,2},{2,1},{1,0},{31,29},{29,30},{30,31},{3,4},{4,3},{5,6},{6,5},... | collective-permute-start | bytes 307208 | tf_op jit(solution)/shard_map/ppermute | solution.py:411
  1.5 7.3 %collective-permute-start.2 = (f32[200,128]{1,0:T(8,128)S(1)}, f32[200,128]{1,0:T(8,128)S(1)}, u32[]{:S(2)}, u32[]{:S(2)}) collective-permute-start(f32[200,128]{1,0:T(8,128)S(1)} %get-tuple-element.28), channel_id=1, source_target_pairs={{1,2},{2,0},{0,3},{3,1},{30,29},{29,31},{31,28},{28,30},{4,6},{5,7... | collective-permute-start | bytes 307208 | tf_op jit(solution)/shard_map/ppermute | solution.py:411
  5.2 4.8 %collective-permute-start = (f32[200,128]{1,0:T(8,128)S(1)}, f32[200,128]{1,0:T(8,128)S(1)}, u32[]{:S(2)}, u32[]{:S(2)}) collective-permute-start(f32[200,128]{1,0:T(8,128)S(1)} %get-tuple-element.27), channel_id=1, source_target_pairs={{0,1},{1,0},{2,3},{3,2},{4,5},{5,4},{6,7},{7,6},{8,9},{9,8},{10,11... | collective-permute-start | bytes 307208 | tf_op jit(solution)/shard_map/ppermute | solution.py:411
  10.0 7.0 %copy-start = (f32[8,128,128]{2,1,0:T(8,128)S(1)}, f32[8,128,128]{2,1,0:T(8,128)}, u32[]{:S(2)}) copy-start(f32[8,128,128]{2,1,0:T(8,128)} %prolong.1) | copy-start | bytes 1572868
  11.9 8.1 %collective-permute-start.3 = (f32[72,128]{1,0:T(8,128)S(1)}, f32[72,128]{1,0:T(8,128)S(1)}, u32[]{:S(2)}, u32[]{:S(2)}) collective-permute-start(f32[72,128]{1,0:T(8,128)S(1)} %get-tuple-element.44.rest_3_), channel_id=1, source_target_pairs={{0,1},{1,0},{2,3},{3,2},{4,5},{5,4},{6,7},{7,6},{8,9},{9,8},{10,11... | collective-permute-start | bytes 110600 | tf_op jit(solution)/shard_map/ppermute | solution.py:411
  14.5 5.6 %collective-permute-start.4 = (f32[72,128]{1,0:T(8,128)S(1)}, f32[72,128]{1,0:T(8,128)S(1)}, u32[]{:S(2)}, u32[]{:S(2)}) collective-permute-start(f32[72,128]{1,0:T(8,128)S(1)} %get-tuple-element.44.rest_3_), channel_id=1, source_target_pairs={{0,2},{2,1},{1,0},{31,29},{29,30},{30,31},{3,4},{4,3},{5,6},{6,5},... | collective-permute-start | bytes 110600 | tf_op jit(solution)/shard_map/ppermute | solution.py:411
  14.5 5.6 %collective-permute-start.5 = (f32[72,128]{1,0:T(8,128)S(1)}, f32[72,128]{1,0:T(8,128)S(1)}, u32[]{:S(2)}, u32[]{:S(2)}) collective-permute-start(f32[72,128]{1,0:T(8,128)S(1)} %get-tuple-element.44.rest_3_), channel_id=1, source_target_pairs={{1,2},{2,0},{0,3},{3,1},{30,29},{29,31},{31,28},{28,30},{4,6},{5,7... | collective-permute-start | bytes 110600 | tf_op jit(solution)/shard_map/ppermute | solution.py:411
  16.2 1.2 %collective-permute-start.6 = (f32[56,128]{1,0:T(8,128)S(1)}, f32[56,128]{1,0:T(8,128)S(1)}, u32[]{:S(2)}, u32[]{:S(2)}) collective-permute-start(f32[56,128]{1,0:T(8,128)S(1)} %get-tuple-element.45), channel_id=1, source_target_pairs={{0,2},{2,0},{1,3},{3,1},{4,6},{6,4},{5,7},{7,5},{8,10},{10,8},{9,1... | collective-permute-start | bytes 86024 | tf_op jit(solution)/shard_map/ppermute | solution.py:411
  16.2 3.9 %collective-permute-start.7 = (f32[56,128]{1,0:T(8,128)S(1)}, f32[56,128]{1,0:T(8,128)S(1)}, u32[]{:S(2)}, u32[]{:S(2)}) collective-permute-start(f32[56,128]{1,0:T(8,128)S(1)} %get-tuple-element.46), channel_id=1, source_target_pairs={{2,4},{4,2},{3,5},{5,3},{6,8},{8,6},{7,9},{9,7},{10,12},{12,10},{1... | collective-permute-start | bytes 86024 | tf_op jit(solution)/shard_map/ppermute | solution.py:411
